TPU v7x, 256 devices: a whole 4x4x8 slice. The times are simulated.
256 devices in a mesh: horiz: 16 (over y, x), depth: 16 (over z, core).
Axes of the slice: x: 4, y: 4, z: 8, core: 2. Of those that a mesh axis runs over, the one named last changes fastest.
Arguments:
- fields: float32 [3, 512, 512, 256], P(None, 'depth', 'horiz'), may hold values from -6 to 6
- diffusivity: float32 [512, 512, 256], P('depth', 'horiz'), may hold values from 0.05 to 0.24
- offsets: int32 [512], P('horiz'), may hold values from 0 to 3
- coupling: float32 [4, 512], P(None, 'depth'), may hold values from 200 to 1600, as said below
- inverse: float32 [4, 512, 32], P(None, 'depth'), as said below
Outputs:
- advanced: float32 [3, 512, 512, 256], P(None, 'depth', 'horiz')
Inputs may be any that keep to these rules, and one draw needn't show every extreme that they name: coupling[o, k] = coupling[0, k + o] wherever both exist. inverse[o, r * 32 + i, j] is entry (i, j) of the inverse of a block matrix: on the levels k of block r it has diagonal 1 + coupling[o, k] + coupling[o, k + 1] (the first term 0 for k = 0, the second 0 for k = 511) and -coupling[o, k] between levels k - 1 and k; in every block, row and column 31 are those of the identity.
All inputs are finite; a program needn't handle non-finite values.
Results may differ from a plain program's by a relative error of at most 0.0003.
Values sent between devices are 32-bit elements; how exact they have to be, the bound alone decides.
A program may use at most 64 MiB of HBM per device.

v0:
```python
import math

import jax
import jax.numpy as jnp
from jax import lax
from jax.sharding import PartitionSpec as P

exact_mode = lax.Precision.HIGHEST
wave_gain = 0.5


def padded_2(block, sides, width):
    for axis, dim in sides:
        count = lax.axis_size(axis)
        forward = [(i, i + 1) for i in range(count - 1)]
        forward.append((count - 1, 0))
        backward = [(target, source) for source, target in forward]
        low = lax.ppermute(
            lax.slice_in_dim(block, block.shape[dim] - width, None, axis=dim), axis, forward
        )
        high = lax.ppermute(lax.slice_in_dim(block, 0, width, axis=dim), axis, backward)
        block = jnp.concatenate([low, block, high], axis=dim)
    return block


def passed_along(block, axis, distance):
    devices = range(lax.axis_size(axis))
    route = [(i - distance, i) for i in devices if i - distance in devices]
    return lax.ppermute(block, axis, route)


def joined_along(parts, dim):
    parts = jnp.moveaxis(parts, 0, dim)
    shape = parts.shape
    return parts.reshape(*shape[:dim], shape[dim] * shape[dim + 1], *shape[dim + 2 :])


def sent_to_all(x, axis):
    copies = jnp.broadcast_to(x, (lax.axis_size(axis), *x.shape))
    return lax.all_to_all(copies, axis, split_axis=0, concat_axis=0, tiled=True)


def collect(x, axis, dim):
    return joined_along(sent_to_all(x, axis), dim)


def sent_together(arrays, axis, dim, along):
    widths = [math.prod(a.shape[along:]) for a in arrays]
    both = jnp.concatenate(
        [a.reshape(*a.shape[:along], w) for a, w in zip(arrays, widths)], axis=along
    )
    out = collect(both, axis, dim)
    parts = jnp.split(out, [sum(widths[:k]) for k in range(1, len(widths))], axis=along)
    return tuple((b.reshape(*out.shape[:along], *a.shape[along:]) for a, b in zip(arrays, parts)))


def tendency(centre, east_side, west_side, diffusivity):
    north_side = jnp.roll(centre, -1, axis=3)
    south_side = jnp.roll(centre, 1, axis=3)
    laplace = east_side + west_side + north_side + south_side - 4.0 * centre
    slope_along = 0.5 * (east_side - west_side)
    slope_across = 0.5 * (north_side - south_side)
    pushed = centre + diffusivity[None] * laplace
    first_part = pushed[0] - wave_gain * slope_along[2]
    second_part = pushed[1] - wave_gain * slope_across[2]
    third_part = pushed[2] - wave_gain * (slope_along[0] + slope_across[1])
    return jnp.stack([first_part, second_part, third_part])


def eliminate(level_slab, inverse_rows, coupling_rows, selector, block_index):
    chosen = jnp.einsum("jo,oab->jab", selector, inverse_rows, precision=exact_mode)
    line_coupling = jnp.dot(selector, coupling_rows, precision=exact_mode)
    solved = jnp.einsum("jab,fbjy->fajy", chosen, level_slab, precision=exact_mode)
    below_face = line_coupling[:, 0]
    upper_gate = line_coupling[:, -1]
    lower_gate = jnp.where(block_index > 0, below_face, jnp.zeros_like(below_face))
    spike_low = chosen[:, :, 0] * lower_gate[:, None]
    spike_high = chosen[:, :, -2] * upper_gate[:, None]
    return (solved, spike_low, spike_high, below_face, upper_gate)


def interface_rows(solved, spike_low, spike_high, upper_gate, got_rows, got_lines):
    lower_band = -upper_gate * spike_low[:, -2]
    main_band = 1.0 + upper_gate + got_lines[0] - upper_gate * spike_high[:, -2] - got_lines[1]
    upper_band = -got_lines[2]
    target = solved[:, -1] + upper_gate[None, :, None] * solved[:, -2] + got_rows
    return (lower_band, main_band, upper_band, target)


def thomas(lower_band, main_band, upper_band, target):

    def forward_step(state_now, row_data):
        prev_ratio, prev_value = state_now
        low_row, main_row, up_row, target_row = row_data
        pivot_value = main_row - low_row * prev_ratio
        ratio_now = up_row / pivot_value
        value_now = (target_row - low_row[None, :, None] * prev_value) / pivot_value[None, :, None]
        return ((ratio_now, value_now), (ratio_now, value_now))

    anchor = jnp.zeros_like(target[0])
    start_ratio = jnp.zeros_like(main_band[0])
    _, (ratios, values) = lax.scan(
        forward_step, (start_ratio, anchor), (lower_band, main_band, upper_band, target)
    )

    def backward_step(next_value, row_data):
        ratio_now, value_now = row_data
        result_now = value_now - ratio_now[None, :, None] * next_value
        return (result_now, result_now)

    _, results = lax.scan(backward_step, anchor, (ratios, values), reverse=True)
    return results


def assemble(solved, spike_low, spike_high, previous, self_value):
    lifted = (
        solved
        + spike_low.T[None, :, :, None] * previous[:, None]
        + spike_high.T[None, :, :, None] * self_value[:, None]
    )
    return jnp.concatenate([lifted[:, :-1], self_value[:, None]], axis=1)


def body(fields, diffusivity, offsets, coupling, inverse):
    padded = padded_2(fields, (("horiz", 2),), 1)
    forcing = tendency(padded[:, :, 1:-1], padded[:, :, 2:], padded[:, :, :-2], diffusivity)
    selector = (offsets[:, None] == jnp.arange(inverse.shape[0], dtype=jnp.int32)[None, :]).astype(
        jnp.float32
    )
    depth_rank = lax.axis_index("depth")
    solved, spike_low, spike_high, below_face, upper_gate = eliminate(
        forcing, inverse, coupling, selector, depth_rank
    )
    send_lines = jnp.stack(
        [below_face, below_face * spike_low[:, 0], below_face * spike_high[:, 0]]
    )
    send_rows = below_face[None, :, None] * solved[:, 0]
    got_rows, got_lines = passed_along((send_rows, send_lines), "depth", -1)
    lower_band, main_band, upper_band, target = interface_rows(
        solved, spike_low, spike_high, upper_gate, got_rows, got_lines
    )
    every_lower, every_main, every_upper, every_target = sent_together(
        (lower_band[None], main_band[None], upper_band[None], target[None]), "depth", 0, 1
    )
    interfaces = thomas(every_lower, every_main, every_upper, every_target)
    self_value = lax.dynamic_index_in_dim(interfaces, depth_rank, 0, keepdims=False)
    previous = lax.dynamic_index_in_dim(
        interfaces, jnp.maximum(depth_rank - 1, 0), 0, keepdims=False
    )
    previous = jnp.where(depth_rank > 0, previous, jnp.zeros_like(previous))
    return assemble(solved, spike_low, spike_high, previous, self_value)


def solution(mesh):
    return jax.shard_map(
        body,
        mesh=mesh,
        in_specs=(
            P(None, "depth", "horiz", None),
            P("depth", "horiz", None),
            P("horiz"),
            P(None, "depth"),
            P(None, "depth", None),
        ),
        out_specs=P(None, "depth", "horiz", None),
        check_vma=False,
    )
```

profile of v0, /device:TPU:1, one launch (start us, length us, event | category | flops | bytes accessed | tf_op | source)
XLA Modules:
  0.0 159.6 jit_solution(1866447706351200701)
XLA Ops:
  0.0 3.7 %copy.109 = f32[3,32,32,256]{3,1,0,2:T(8,128)S(1)} copy(f32[3,32,32,256]{3,2,1,0:T(8,128)} %param.9) | data formatting | bytes 6291456 | tf_op args[0]
  4.4 5.7 %collective-permute-start = (f32[3,32,1,256]{3,1,0,2:T(8,128)}, f32[3,32,1,256]{3,1,0,2:T(8,128)S(1)}, u32[]{:S(2)}, u32[]{:S(2)}) collective-permute-start(f32[3,32,1,256]{3,1,0,2:T(8,128)} %get-tuple-element.251), channel_id=1, source_target_pairs={{16,0},{32,16},{48,32},{64,48},{80,64},{96,80},{112,96},{128,112},... | collective-permute-start | bytes 294920 | tf_op jit(solution)/shard_map/ppermute | solution.py:21
  15.4 3.0 %collective-permute-start.2 = (f32[3,32]{1,0:T(4,128)}, f32[3,32]{1,0:T(4,128)S(1)}, u32[]{:S(2)}, u32[]{:S(2)}) collective-permute-start(f32[3,32]{1,0:T(4,128)} %pad_maximum_fusion.5), channel_id=1, source_target_pairs={{1,0},{2,1},{3,2},{4,3},{5,4},{6,5},{7,6},{8,7},{9,8},{10,9},{11,1... | collective-permute-start | bytes 1160 | tf_op jit(solution)/shard_map/ppermute | solution.py:29
  18.4 4.0 %fusion.43 = (f32[3,32,32,255]{3,1,0,2:T(8,128)}, f32[3,32,32,255]{3,1,0,2:T(8,128)}) fusion(f32[3,32,32,256]{3,1,0,2:T(8,128)S(1)} %copy.109), kind=kLoop, calls=%fused_computation.81 | loop fusion | bytes 12533760 | tf_op jit(solution)/shard_map/jit(_roll_static)/slice | solution.py:58
  22.4 2.2 %fusion.44 = (f32[3,32,32,1]{3,1,0,2:T(8,128)}, f32[3,32,32,1]{3,1,0,2:T(8,128)}) fusion(f32[3,32,32,256]{3,1,0,2:T(8,128)S(1)} %copy.109), kind=kLoop, calls=%fused_computation.82 | loop fusion | bytes 49152 | tf_op jit(solution)/shard_map/jit(_roll_static)/slice | solution.py:58
  26.2 2.3 %copy.122 = f32[32,32,32,1]{2,1,3,0:T(8,128)} copy(f32[32,32,32,1]{0,2,1,3:T(8,128)} %bitcast.117) | data formatting | bytes 262144 | tf_op jit(solution)/shard_map/jo,oab->jab/dot_general | solution.py:71
  28.5 5.3 %multiply_add_fusion = (f32[3,32,32,256]{3,1,0,2:T(8,128)S(1)}, f32[3,32,32,256]{3,1,0,2:T(8,128)S(1)}, f32[3,32,32,256]{3,1,0,2:T(8,128)S(1)}) fusion(f32[3,32,32,256]{3,1,0,2:T(8,128)S(1)} %copy.109, f32[3,32,1,256]{3,1,0,2:T(8,128)S(1)} %collective-permute-done, f32[3,32,1,256]{3,1,0,2:T(8,128)S(1)} %collective-permute-done.1, ...), kind=kLoop, calls=%fused_computation.34 | loop fusion | flops 11796480 | bytes 20119552 | tf_op jit(solution)/shard_map/add | solution.py:63
  34.8 2.9 %fusion.15 = f32[3,32,32,256]{3,1,0,2:T(8,128)S(1)} fusion(f32[32,32,32,1]{2,1,3,0:T(8,128)S(1)} %copy-done.2, f32[1,32,32,256]{3,1,0,2:T(8,128)S(1)} %get-tuple-element.244, f32[1,32,32,256]{3,1,0,2:T(8,128)S(1)} %get-tuple-element.245, f32[1,32,32,256]{3,1,0,2:T(8,128)S(1)} %get-tuple-element.243), kind=kOutput, calls=%fused_computation.35 | convolution fusion | flops 303562752 | bytes 6422528 | tf_op jit(solution)/shard_map/jab,fbjy->fajy/dot_general | solution.py:73
  38.0 1.9 %collective-permute-start.3 = (f32[3,32,256]{2,1,0:T(8,128)S(1)}, f32[3,32,256]{2,1,0:T(8,128)S(1)}, u32[]{:S(2)}, u32[]{:S(2)}) collective-permute-start(f32[3,32,256]{2,1,0:T(8,128)S(1)} %bitcast_multiply_fusion), channel_id=1, source_target_pairs={{1,0},{2,1},{3,2},{4,3},{5,4},{6,5},{7,6},{8,7},{9,8},{10,9},{11,1... | collective-permute-start | bytes 294920 | tf_op jit(solution)/shard_map/ppermute | solution.py:29
  40.6 3.3 %collective-permute-done.3 = f32[3,32,256]{2,1,0:T(8,128)S(1)} collective-permute-done((f32[3,32,256]{2,1,0:T(8,128)S(1)}, f32[3,32,256]{2,1,0:T(8,128)S(1)}, u32[]{:S(2)}, u32[]{:S(2)}) %collective-permute-start.3) | collective-permute-done | bytes 98336 | tf_op jit(solution)/shard_map/ppermute | solution.py:29
  44.8 2.0 %broadcast_in_dim.41 = f32[16,1,24672]{2,1,0:T(1,128)} broadcast(f32[24672]{0:T(1024)S(1)} %reduce), dimensions={2} | broadcast | bytes 1677696 | tf_op jit(solution)/shard_map/broadcast_in_dim | solution.py:39
  46.7 8.6 %all-to-all-start = ((f32[16,1,24672]{2,1,0:T(1,128)}), f32[16,1,24672]{2,1,0:T(1,128)}, u32[]{:S(2)}, u32[]{:S(2)}) async-start(f32[16,1,24672]{2,1,0:T(1,128)} %broadcast_in_dim.41), calls=%async_computation | async-start | bytes 3162112 | tf_op jit(solution)/shard_map/all_to_all | solution.py:40
  55.5 38.6 %all-to-all-done = f32[16,1,24672]{2,1,0:T(1,128)} async-done(((f32[16,1,24672]{2,1,0:T(1,128)}), f32[16,1,24672]{2,1,0:T(1,128)}, u32[]{:S(2)}, u32[]{:S(2)}) %all-to-all-start) | async-done | bytes 1579040 | tf_op jit(solution)/shard_map/all_to_all | solution.py:40
  99.2 27.3 %while.34 = (s32[]{:T(128)}, f32[32]{0:T(128)S(1)}, f32[3,32,256]{2,1,0:T(8,128)S(1)}, f32[16,32]{1,0:T(8,128)S(1)}, f32[16,3,32,256]{3,2,1,0:T(8,128)}, /*index...) while((s32[]{:T(128)}, f32[32]{0:T(128)S(1)}, ...), condition=%wide.region_1.2_spmd.clone, body=%wide.region_0.1_spmd.clone.sunk | while | flops 98435 | bytes 395396 | solution.py:102
  99.2 1.6 %bitcast_dynamic-update-slice_fusion.4 = (f32[16,3,32,256]{3,2,1,0:T(8,128)}, f32[3,32,256]{2,1,0:T(8,128)S(1)}) fusion(f32[16,3,32,256]{3,2,1,0:T(8,128)} %get-tuple-element.385, s32[]{:T(128)} %get-tuple-element.381, f32[32]{0:T(128)S(1)} %get-tuple-element.360, f32[3,32,256]{2,1,0:T(8,128)S(1)} %get-tuple-element.383, pred[]{:T(512)S(6)} %compare.6, ...), kind=kLoop, calls=%fused_computation.clone.1 | loop fusion | flops 98304 | bytes 393985 | tf_op jit(solution)/shard_map/while/body/jit(dynamic_update_index_in_dim)/dynamic_update_slice | solution.py:102
  100.9 1.6 %bitcast_dynamic-update-slice_fusion.4 = (f32[16,3,32,256]{3,2,1,0:T(8,128)}, f32[3,32,256]{2,1,0:T(8,128)S(1)}) fusion(f32[16,3,32,256]{3,2,1,0:T(8,128)} %get-tuple-element.385, s32[]{:T(128)} %get-tuple-element.381, f32[32]{0:T(128)S(1)} %get-tuple-element.360, f32[3,32,256]{2,1,0:T(8,128)S(1)} %get-tuple-element.383, pred[]{:T(512)S(6)} %compare.6, ...), kind=kLoop, calls=%fused_computation.clone.1 | loop fusion | flops 98304 | bytes 393985 | tf_op jit(solution)/shard_map/while/body/jit(dynamic_update_index_in_dim)/dynamic_update_slice | solution.py:102
  102.6 1.6 %bitcast_dynamic-update-slice_fusion.4 = (f32[16,3,32,256]{3,2,1,0:T(8,128)}, f32[3,32,256]{2,1,0:T(8,128)S(1)}) fusion(f32[16,3,32,256]{3,2,1,0:T(8,128)} %get-tuple-element.385, s32[]{:T(128)} %get-tuple-element.381, f32[32]{0:T(128)S(1)} %get-tuple-element.360, f32[3,32,256]{2,1,0:T(8,128)S(1)} %get-tuple-element.383, pred[]{:T(512)S(6)} %compare.6, ...), kind=kLoop, calls=%fused_computation.clone.1 | loop fusion | flops 98304 | bytes 393985 | tf_op jit(solution)/shard_map/while/body/jit(dynamic_update_index_in_dim)/dynamic_update_slice | solution.py:102
  104.3 1.6 %bitcast_dynamic-update-slice_fusion.4 = (f32[16,3,32,256]{3,2,1,0:T(8,128)}, f32[3,32,256]{2,1,0:T(8,128)S(1)}) fusion(f32[16,3,32,256]{3,2,1,0:T(8,128)} %get-tuple-element.385, s32[]{:T(128)} %get-tuple-element.381, f32[32]{0:T(128)S(1)} %get-tuple-element.360, f32[3,32,256]{2,1,0:T(8,128)S(1)} %get-tuple-element.383, pred[]{:T(512)S(6)} %compare.6, ...), kind=kLoop, calls=%fused_computation.clone.1 | loop fusion | flops 98304 | bytes 393985 | tf_op jit(solution)/shard_map/while/body/jit(dynamic_update_index_in_dim)/dynamic_update_slice | solution.py:102
  106.0 1.6 %bitcast_dynamic-update-slice_fusion.4 = (f32[16,3,32,256]{3,2,1,0:T(8,128)}, f32[3,32,256]{2,1,0:T(8,128)S(1)}) fusion(f32[16,3,32,256]{3,2,1,0:T(8,128)} %get-tuple-element.385, s32[]{:T(128)} %get-tuple-element.381, f32[32]{0:T(128)S(1)} %get-tuple-element.360, f32[3,32,256]{2,1,0:T(8,128)S(1)} %get-tuple-element.383, pred[]{:T(512)S(6)} %compare.6, ...), kind=kLoop, calls=%fused_computation.clone.1 | loop fusion | flops 98304 | bytes 393985 | tf_op jit(solution)/shard_map/while/body/jit(dynamic_update_index_in_dim)/dynamic_update_slice | solution.py:102
  107.7 1.6 %bitcast_dynamic-update-slice_fusion.4 = (f32[16,3,32,256]{3,2,1,0:T(8,128)}, f32[3,32,256]{2,1,0:T(8,128)S(1)}) fusion(f32[16,3,32,256]{3,2,1,0:T(8,128)} %get-tuple-element.385, s32[]{:T(128)} %get-tuple-element.381, f32[32]{0:T(128)S(1)} %get-tuple-element.360, f32[3,32,256]{2,1,0:T(8,128)S(1)} %get-tuple-element.383, pred[]{:T(512)S(6)} %compare.6, ...), kind=kLoop, calls=%fused_computation.clone.1 | loop fusion | flops 98304 | bytes 393985 | tf_op jit(solution)/shard_map/while/body/jit(dynamic_update_index_in_dim)/dynamic_update_slice | solution.py:102
  109.4 1.6 %bitcast_dynamic-update-slice_fusion.4 = (f32[16,3,32,256]{3,2,1,0:T(8,128)}, f32[3,32,256]{2,1,0:T(8,128)S(1)}) fusion(f32[16,3,32,256]{3,2,1,0:T(8,128)} %get-tuple-element.385, s32[]{:T(128)} %get-tuple-element.381, f32[32]{0:T(128)S(1)} %get-tuple-element.360, f32[3,32,256]{2,1,0:T(8,128)S(1)} %get-tuple-element.383, pred[]{:T(512)S(6)} %compare.6, ...), kind=kLoop, calls=%fused_computation.clone.1 | loop fusion | flops 98304 | bytes 393985 | tf_op jit(solution)/shard_map/while/body/jit(dynamic_update_index_in_dim)/dynamic_update_slice | solution.py:102
  111.1 1.6 %bitcast_dynamic-update-slice_fusion.4 = (f32[16,3,32,256]{3,2,1,0:T(8,128)}, f32[3,32,256]{2,1,0:T(8,128)S(1)}) fusion(f32[16,3,32,256]{3,2,1,0:T(8,128)} %get-tuple-element.385, s32[]{:T(128)} %get-tuple-element.381, f32[32]{0:T(128)S(1)} %get-tuple-element.360, f32[3,32,256]{2,1,0:T(8,128)S(1)} %get-tuple-element.383, pred[]{:T(512)S(6)} %compare.6, ...), kind=kLoop, calls=%fused_computation.clone.1 | loop fusion | flops 98304 | bytes 393985 | tf_op jit(solution)/shard_map/while/body/jit(dynamic_update_index_in_dim)/dynamic_update_slice | solution.py:102
  112.8 1.6 %bitcast_dynamic-update-slice_fusion.4 = (f32[16,3,32,256]{3,2,1,0:T(8,128)}, f32[3,32,256]{2,1,0:T(8,128)S(1)}) fusion(f32[16,3,32,256]{3,2,1,0:T(8,128)} %get-tuple-element.385, s32[]{:T(128)} %get-tuple-element.381, f32[32]{0:T(128)S(1)} %get-tuple-element.360, f32[3,32,256]{2,1,0:T(8,128)S(1)} %get-tuple-element.383, pred[]{:T(512)S(6)} %compare.6, ...), kind=kLoop, calls=%fused_computation.clone.1 | loop fusion | flops 98304 | bytes 393985 | tf_op jit(solution)/shard_map/while/body/jit(dynamic_update_index_in_dim)/dynamic_update_slice | solution.py:102
  114.5 1.6 %bitcast_dynamic-update-slice_fusion.4 = (f32[16,3,32,256]{3,2,1,0:T(8,128)}, f32[3,32,256]{2,1,0:T(8,128)S(1)}) fusion(f32[16,3,32,256]{3,2,1,0:T(8,128)} %get-tuple-element.385, s32[]{:T(128)} %get-tuple-element.381, f32[32]{0:T(128)S(1)} %get-tuple-element.360, f32[3,32,256]{2,1,0:T(8,128)S(1)} %get-tuple-element.383, pred[]{:T(512)S(6)} %compare.6, ...), kind=kLoop, calls=%fused_computation.clone.1 | loop fusion | flops 98304 | bytes 393985 | tf_op jit(solution)/shard_map/while/body/jit(dynamic_update_index_in_dim)/dynamic_update_slice | solution.py:102
  116.2 1.6 %bitcast_dynamic-update-slice_fusion.4 = (f32[16,3,32,256]{3,2,1,0:T(8,128)}, f32[3,32,256]{2,1,0:T(8,128)S(1)}) fusion(f32[16,3,32,256]{3,2,1,0:T(8,128)} %get-tuple-element.385, s32[]{:T(128)} %get-tuple-element.381, f32[32]{0:T(128)S(1)} %get-tuple-element.360, f32[3,32,256]{2,1,0:T(8,128)S(1)} %get-tuple-element.383, pred[]{:T(512)S(6)} %compare.6, ...), kind=kLoop, calls=%fused_computation.clone.1 | loop fusion | flops 98304 | bytes 393985 | tf_op jit(solution)/shard_map/while/body/jit(dynamic_update_index_in_dim)/dynamic_update_slice | solution.py:102
  117.9 1.6 %bitcast_dynamic-update-slice_fusion.4 = (f32[16,3,32,256]{3,2,1,0:T(8,128)}, f32[3,32,256]{2,1,0:T(8,128)S(1)}) fusion(f32[16,3,32,256]{3,2,1,0:T(8,128)} %get-tuple-element.385, s32[]{:T(128)} %get-tuple-element.381, f32[32]{0:T(128)S(1)} %get-tuple-element.360, f32[3,32,256]{2,1,0:T(8,128)S(1)} %get-tuple-element.383, pred[]{:T(512)S(6)} %compare.6, ...), kind=kLoop, calls=%fused_computation.clone.1 | loop fusion | flops 98304 | bytes 393985 | tf_op jit(solution)/shard_map/while/body/jit(dynamic_update_index_in_dim)/dynamic_update_slice | solution.py:102
  119.6 1.6 %bitcast_dynamic-update-slice_fusion.4 = (f32[16,3,32,256]{3,2,1,0:T(8,128)}, f32[3,32,256]{2,1,0:T(8,128)S(1)}) fusion(f32[16,3,32,256]{3,2,1,0:T(8,128)} %get-tuple-element.385, s32[]{:T(128)} %get-tuple-element.381, f32[32]{0:T(128)S(1)} %get-tuple-element.360, f32[3,32,256]{2,1,0:T(8,128)S(1)} %get-tuple-element.383, pred[]{:T(512)S(6)} %compare.6, ...), kind=kLoop, calls=%fused_computation.clone.1 | loop fusion | flops 98304 | bytes 393985 | tf_op jit(solution)/shard_map/while/body/jit(dynamic_update_index_in_dim)/dynamic_update_slice | solution.py:102
  121.3 1.6 %bitcast_dynamic-update-slice_fusion.4 = (f32[16,3,32,256]{3,2,1,0:T(8,128)}, f32[3,32,256]{2,1,0:T(8,128)S(1)}) fusion(f32[16,3,32,256]{3,2,1,0:T(8,128)} %get-tuple-element.385, s32[]{:T(128)} %get-tuple-element.381, f32[32]{0:T(128)S(1)} %get-tuple-element.360, f32[3,32,256]{2,1,0:T(8,128)S(1)} %get-tuple-element.383, pred[]{:T(512)S(6)} %compare.6, ...), kind=kLoop, calls=%fused_computation.clone.1 | loop fusion | flops 98304 | bytes 393985 | tf_op jit(solution)/shard_map/while/body/jit(dynamic_update_index_in_dim)/dynamic_update_slice | solution.py:102
  123.1 1.6 %bitcast_dynamic-update-slice_fusion.4 = (f32[16,3,32,256]{3,2,1,0:T(8,128)}, f32[3,32,256]{2,1,0:T(8,128)S(1)}) fusion(f32[16,3,32,256]{3,2,1,0:T(8,128)} %get-tuple-element.385, s32[]{:T(128)} %get-tuple-element.381, f32[32]{0:T(128)S(1)} %get-tuple-element.360, f32[3,32,256]{2,1,0:T(8,128)S(1)} %get-tuple-element.383, pred[]{:T(512)S(6)} %compare.6, ...), kind=kLoop, calls=%fused_computation.clone.1 | loop fusion | flops 98304 | bytes 393985 | tf_op jit(solution)/shard_map/while/body/jit(dynamic_update_index_in_dim)/dynamic_update_slice | solution.py:102
  124.8 1.6 %bitcast_dynamic-update-slice_fusion.4 = (f32[16,3,32,256]{3,2,1,0:T(8,128)}, f32[3,32,256]{2,1,0:T(8,128)S(1)}) fusion(f32[16,3,32,256]{3,2,1,0:T(8,128)} %get-tuple-element.385, s32[]{:T(128)} %get-tuple-element.381, f32[32]{0:T(128)S(1)} %get-tuple-element.360, f32[3,32,256]{2,1,0:T(8,128)S(1)} %get-tuple-element.383, pred[]{:T(512)S(6)} %compare.6, ...), kind=kLoop, calls=%fused_computation.clone.1 | loop fusion | flops 98304 | bytes 393985 | tf_op jit(solution)/shard_map/while/body/jit(dynamic_update_index_in_dim)/dynamic_update_slice | solution.py:102
  127.8 26.0 %while.35 = (s32[]{:T(128)}, f32[3,32,256]{2,1,0:T(8,128)S(1)}, f32[16,3,32,256]{3,2,1,0:T(8,128)}, f32[16,3,32,256]{3,2,1,0:T(8,128)}, f32[16,32]{1,0:T(8,128)S(1)}, /*index=5*/s32[]{:T(128)}, s32[]{:T(128)}, s32[]{:T(128)}) while((s32[]{:T(128)}, f32[3,32,256]{2,1,0:T(8,128)S(1)}, f32[16,3,32,256]{3,2,1,0:T(8,128)}, ...), condition=%wide.region_3.4_spmd.clone, body=%wide.region_2.3_spmd.clone.sunk | while | flops 73732 | bytes 393715 | solution.py:111
  156.1 3.5 %copy.121 = f32[3,32,32,256]{3,2,1,0:T(8,128)} copy(f32[3,32,32,256]{3,1,0,2:T(8,128)S(1)} %pad_maximum_fusion.4) | data formatting | bytes 6291456 | tf_op jit(solution)/shard_map/concatenate | solution.py:121
  (139 shorter events, 46.0 us)
Async XLA Ops:
  0.0 10.2 %copy-start = (f32[4,32,32]{2,1,0:T(8,128)S(1)}, f32[4,32,32]{2,1,0:T(8,128)}, u32[]{:S(2)}) copy-start(f32[4,32,32]{2,1,0:T(8,128)} %param.13) | copy-start | bytes 49156
  0.0 10.2 %copy-start.6 = (s32[32]{0:T(128)S(1)}, s32[32]{0:T(128)}, u32[]{:S(2)}) copy-start(s32[32]{0:T(128)} %param.11) | copy-start | bytes 388
  0.0 10.8 %copy-start.7 = (f32[4,32]{1,0:T(4,128)S(1)}, f32[4,32]{1,0:T(4,128)}, u32[]{:S(2)}) copy-start(f32[4,32]{1,0:T(4,128)} %param.12) | copy-start | bytes 1540
  4.4 24.1 %collective-permute-start = (f32[3,32,1,256]{3,1,0,2:T(8,128)}, f32[3,32,1,256]{3,1,0,2:T(8,128)S(1)}, u32[]{:S(2)}, u32[]{:S(2)}) collective-permute-start(f32[3,32,1,256]{3,1,0,2:T(8,128)} %get-tuple-element.251), channel_id=1, source_target_pairs={{16,0},{32,16},{48,32},{64,48},{80,64},{96,80},{112,96},{128,112},... | collective-permute-start | bytes 294920 | tf_op jit(solution)/shard_map/ppermute | solution.py:21
  10.2 18.3 %collective-permute-start.1 = (f32[3,32,1,256]{3,1,0,2:T(8,128)S(1)}, f32[3,32,1,256]{3,1,0,2:T(8,128)S(1)}, u32[]{:S(2)}, u32[]{:S(2)}) collective-permute-start(f32[3,32,1,256]{3,1,0,2:T(8,128)S(1)} %get-tuple-element.250), channel_id=1, source_target_pairs={{0,16},{16,32},{32,48},{48,64},{64,80},{80,96},{96,112},{112,128},... | collective-permute-start | bytes 294920 | tf_op jit(solution)/shard_map/ppermute | solution.py:18
  10.8 0.8 copy-start.1
  13.6 0.6 copy-start.4
  15.4 24.5 %collective-permute-start.2 = (f32[3,32]{1,0:T(4,128)}, f32[3,32]{1,0:T(4,128)S(1)}, u32[]{:S(2)}, u32[]{:S(2)}) collective-permute-start(f32[3,32]{1,0:T(4,128)} %pad_maximum_fusion.5), channel_id=1, source_target_pairs={{1,0},{2,1},{3,2},{4,3},{5,4},{6,5},{7,6},{8,7},{9,8},{10,9},{11,1... | collective-permute-start | bytes 1160 | tf_op jit(solution)/shard_map/ppermute | solution.py:29
  22.4 2.2 %copy-start.3 = (f32[32,32,256]{2,1,0:T(8,128)S(1)}, f32[32,32,256]{2,1,0:T(8,128)}, u32[]{:S(2)}) copy-start(f32[32,32,256]{2,1,0:T(8,128)} %param.10) | copy-start | bytes 3145732
  33.8 1.0 copy-start.2
  34.8 9.3 %copy-start.5 = (f32[1,32]{1,0:T(1,128)S(1)}, f32[1,32]{1,0:T(1,128)}, u32[]{:S(2)}) copy-start(f32[1,32]{1,0:T(1,128)} %get-tuple-element.267) | copy-start | bytes 388
  38.0 5.9 %collective-permute-start.3 = (f32[3,32,256]{2,1,0:T(8,128)S(1)}, f32[3,32,256]{2,1,0:T(8,128)S(1)}, u32[]{:S(2)}, u32[]{:S(2)}) collective-permute-start(f32[3,32,256]{2,1,0:T(8,128)S(1)} %bitcast_multiply_fusion), channel_id=1, source_target_pairs={{1,0},{2,1},{3,2},{4,3},{5,4},{6,5},{7,6},{8,7},{9,8},{10,9},{11,1... | collective-permute-start | bytes 294920 | tf_op jit(solution)/shard_map/ppermute | solution.py:29
  46.7 47.4 %all-to-all-start = ((f32[16,1,24672]{2,1,0:T(1,128)}), f32[16,1,24672]{2,1,0:T(1,128)}, u32[]{:S(2)}, u32[]{:S(2)}) async-start(f32[16,1,24672]{2,1,0:T(1,128)} %broadcast_in_dim.41), calls=%async_computation | async-start | bytes 3162112 | tf_op jit(solution)/shard_map/all_to_all | solution.py:40
where the time goes:
time: 161 us; the launch traced here: 160 us
  other arithmetic  64.7 us (40%)
  waiting for transfers between devices  41.9 us (26%)
  local copies, waits for them, and re-layouts  28.9 us (18%)
  starting transfers between devices  19.3 us (12%)
  matrix products  4.28 us (3%)
    dynamic_update_slice x32, other arithmetic, thomas(): lax.scan(forward_step, (start_ratio, anchor), (lower_band, main_band, upp...  52 us
    all_to_all x1, waiting for transfers between devices, sent_to_all(): return lax.all_to_all(copies, axis, split_axis=0, concat_axis=0, tiled=True)  38.6 us
    unnamed x22, local copies, waits for them, and re-layouts  9.43 us
    all_to_all x1, starting transfers between devices, sent_to_all(): return lax.all_to_all(copies, axis, split_axis=0, concat_axis=0, tiled=True)  8.59 us
    slice x2, local copies, waits for them, and re-layouts, tendency(): north_side = jnp.roll(centre, -1, axis=3)  6.18 us
    ppermute x1, starting transfers between devices, padded_2(): lax.ppermute(lax.slice_in_dim(block, 0, width, axis=dim), axis, backward)  5.75 us
    add x1, other arithmetic, tendency(): pushed = centre + diffusivity[None] * laplace  5.3 us
    ppermute x2, starting transfers between devices, passed_along(): return lax.ppermute(block, axis, route)  4.94 us
  transfers between devices with their start and end apart: 5, of which 2 were waited for; matrix products, arithmetic and copies ran while one was open for 16% of the time, Pallas kernels for 0%

commit v1 on v0

v1 whole, which is shorter than its diff:
```python
import functools

import jax
import jax.numpy as jnp
from jax import lax
from jax.experimental import pallas as pl
from jax.experimental.pallas import tpu as pltpu
from jax.sharding import PartitionSpec as P

MESH = pl.DeviceIdType.MESH
CHUNKS = 4
PAD = 48
LINES = 32
MSG = 24


def depth_order(n):
    half = n // 2
    steps = sorted(range(half), key=lambda s: -min(s, half - s))
    return [(s, c) for s in steps for c in (0, 1) if (s, c) != (0, 0)]


def solve_kernel(
    n_h, n_d,
    fields, diff, offs, coup, inv,
    sol, back, low, high,
    fbuf, dbuf, offv, cvec, kvec, wv, iv, acc, delta,
    hsend, hrecv, cmsg, crecv, m1, r1, m2,
    load_sem, small_sem, hs_sem, hr_sem, cs_sem, cr_sem, s1_sem, r1_sem, s2_sem, r2_sem,
):
    f32 = jnp.float32
    levels = fields.shape[1]
    per = levels // CHUNKS
    me_h = lax.axis_index("horiz")
    me = lax.axis_index("depth")
    east = lax.rem(me_h + 1, n_h)
    west = lax.rem(me_h + n_h - 1, n_h)

    small = [
        pltpu.make_async_copy(offs, offv, small_sem.at[0]),
        pltpu.make_async_copy(coup, cvec, small_sem.at[1]),
        pltpu.make_async_copy(inv, kvec, small_sem.at[2]),
    ]
    for copy in small:
        copy.start()

    def chunk_copies(c):
        lev = pl.ds(c * per, per)
        out = []
        for h in range(2):
            lane = pl.ds(h * 128, 128)
            for f in range(3):
                out.append(pltpu.make_async_copy(
                    fields.at[f, lev, :, lane],
                    fbuf.at[lev, h * 3 + f, pl.ds(8, LINES), :],
                    load_sem.at[c, h * 3 + f]))
            out.append(pltpu.make_async_copy(
                diff.at[lev, :, lane], dbuf.at[lev, h], load_sem.at[c, 6 + h]))
        return out

    for c in range(CHUNKS):
        for copy in chunk_copies(c):
            copy.start()

    barrier = pltpu.get_barrier_semaphore()
    for to in (east, west):
        pl.semaphore_signal(barrier, inc=1, device_id=(to, me), device_id_type=MESH)
    z, core = me // 2, lax.rem(me, 2)

    def peer_at(step, flip):
        zz = lax.rem(z + step, n_d // 2)
        cc = core if flip == 0 else 1 - core
        return zz * 2 + cc

    order = depth_order(n_d)
    for step, flip in order:
        pl.semaphore_signal(barrier, inc=1, device_id=(me_h, peer_at(step, flip)), device_id_type=MESH)

    f2 = fbuf.reshape(levels * 6 * PAD, 128)
    f2[pl.ds(7, levels * 6, stride=PAD), :] = jnp.zeros((levels * 6, 128), f32)
    f2[pl.ds(40, levels * 6, stride=PAD), :] = jnp.zeros((levels * 6, 128), f32)
    for e in range(2):
        hrecv[e, 0:8, :] = jnp.zeros((8, 128), f32)
        hrecv[e, 200:208, :] = jnp.zeros((8, 128), f32)
    acc[...] = jnp.zeros(acc.shape, f32)

    for copy in small:
        copy.wait()
    sub = lax.broadcasted_iota(jnp.int32, (8, 128), 0)
    lane8 = lax.broadcasted_iota(jnp.int32, (8, 128), 1)
    offset_of = []
    for g in range(4):
        v = jnp.full((8, 128), offv[8 * g], jnp.int32)
        for i in range(1, 8):
            v = jnp.where(sub == i, offv[8 * g + i], v)
        offset_of.append(v)
    masks = [[offset_of[g] == o for o in range(3)] for g in range(4)]

    couple = cvec[...]
    first_row = kvec[:, 0, :]
    last_row = kvec[:, levels - 2, :]
    c_low = jnp.broadcast_to(couple[:, 0:1], (4, levels))
    c_high = jnp.broadcast_to(couple[:, levels - 1:levels], (4, levels))
    gate = jnp.where(me > 0, 1.0, 0.0).astype(f32)
    table_low = first_row * (c_low * gate)
    table_high = last_row * c_high

    def column(table, k):
        return jnp.broadcast_to(table[:, k:k + 1], (4, 128))

    def spread(table4, g):
        rows = [jnp.broadcast_to(table4[o:o + 1, :], (8, 128)) for o in range(4)]
        m = masks[g]
        return jnp.where(m[0], rows[0], jnp.where(m[1], rows[1], jnp.where(m[2], rows[2], rows[3])))

    highs = []
    lows = []
    for k in range(levels):
        lo = column(table_low, k)
        hi = column(table_high, k) if k < levels - 1 else jnp.ones((4, 128), f32)
        if k == levels - 1:
            lo = jnp.zeros((4, 128), f32)
        lows.append(lo)
        highs.append(hi)
        for g in range(4):
            low[k, 8 * g:8 * g + 8, :] = spread(lo, g)
            high[k, 8 * g:8 * g + 8, :] = spread(hi, g)

    c_low4 = jnp.broadcast_to(couple[:, 0:1], (4, 128))
    c_high4 = jnp.broadcast_to(couple[:, levels - 1:levels], (4, 128))
    alpha = c_high4 - c_high4 * highs[levels - 2]
    beta = c_low4 - c_low4 * lows[0]
    cross = c_high4 * lows[levels - 2]
    lane4 = lax.broadcasted_iota(jnp.int32, (4, 128), 1)
    packed = jnp.where(lane4 < 32, alpha, jnp.where(lane4 < 64, beta, cross))
    cmsg[0:4, :] = packed
    cmsg[4:8, :] = packed

    lane = lane8
    is_last = lane == 127
    is_first = lane == 0

    def arrived(c):
        for copy in chunk_copies(c):
            copy.wait()

    def forcing_chunk(c):
        for g in range(4):
            r0 = 8 + 8 * g
            sums = [acc[w, q, 8 * g:8 * g + 8, :] for w in range(2) for q in range(6)]
            for l in range(per):
                k = c * per + l
                hi = high[k, 8 * g:8 * g + 8, :]
                lo = low[k, 8 * g:8 * g + 8, :]
                mid = [fbuf[k, q, r0:r0 + 8, :] for q in range(6)]
                es = [fbuf[k, q, r0 + 1:r0 + 9, :] for q in range(6)]
                ws = [fbuf[k, q, r0 - 1:r0 + 7, :] for q in range(6)]
                up = [pltpu.roll(mid[q], 127, 1) for q in range(6)]
                dn = [pltpu.roll(mid[q], 1, 1) for q in range(6)]
                for h in range(2):
                    d = dbuf[k, h, 8 * g:8 * g + 8, :]
                    keep = 1.0 - 4.0 * d
                    q = [h * 3 + f for f in range(3)]
                    qo = [(1 - h) * 3 + f for f in range(3)]
                    north = [jnp.where(is_last, up[qo[f]], up[q[f]]) for f in range(3)]
                    south = [jnp.where(is_first, dn[qo[f]], dn[q[f]]) for f in range(3)]
                    base = [
                        mid[q[f]] * keep + d * ((es[q[f]] + ws[q[f]]) + (north[f] + south[f]))
                        for f in range(3)
                    ]
                    out = [
                        base[0] - 0.25 * (es[q[2]] - ws[q[2]]),
                        base[1] - 0.25 * (north[2] - south[2]),
                        base[2] - 0.25 * ((es[q[0]] - ws[q[0]]) + (north[1] - south[1])),
                    ]
                    for f in range(3):
                        sol[k, q[f], 8 * g:8 * g + 8, :] = out[f]
                        sums[q[f]] = sums[q[f]] + hi * out[f]
                        sums[6 + q[f]] = sums[6 + q[f]] + lo * out[f]
            for w in range(2):
                for q in range(6):
                    acc[w, q, 8 * g:8 * g + 8, :] = sums[w * 6 + q]

    def chunk_step(c, carry):
        arrived(c)
        forcing_chunk(c)
        return carry

    lax.fori_loop(0, CHUNKS - 1, chunk_step, 0)
    arrived(CHUNKS - 1)

    pl.semaphore_wait(barrier, 2 + len(order))
    hsend[0] = f2[pl.ds(39, levels * 6, stride=PAD), :]
    hsend[1] = f2[pl.ds(8, levels * 6, stride=PAD), :]
    coef_copies = []
    for j, (step, flip) in enumerate(order):
        peer = peer_at(step, flip)
        coef_copies.append(pltpu.make_async_remote_copy(
            src_ref=cmsg, dst_ref=crecv.at[me], send_sem=cs_sem.at[j], recv_sem=cr_sem.at[me],
            device_id=(me_h, peer), device_id_type=MESH))
    halo = []
    for e, to in ((0, east), (1, west)):
        halo.append(pltpu.make_async_remote_copy(
            src_ref=hsend.at[e], dst_ref=hrecv.at[e, pl.ds(8, levels * 6), :],
            send_sem=hs_sem.at[e], recv_sem=hr_sem.at[e],
            device_id=(to, me), device_id_type=MESH))
    for copy in halo:
        copy.start()
    for copy in coef_copies:
        copy.start()
    forcing_chunk(CHUNKS - 1)

    m1r = m1.reshape(n_d * MSG, 128)

    def row_of(f, which, slot, h):
        return f * 8 + which * 4 + slot * 2 + h

    for g in range(4):
        p0, slot = 8 * (g % 2), g // 2
        for w in range(2):
            for h in range(2):
                for f in range(3):
                    m1r[pl.ds(p0 * MSG + row_of(f, w, slot, h), 8, stride=MSG), :] = acc[
                        w, h * 3 + f, 8 * g:8 * g + 8, :]

    def message(j, peer):
        return pltpu.make_async_remote_copy(
            src_ref=m1.at[peer], dst_ref=r1.at[me], send_sem=s1_sem.at[j], recv_sem=r1_sem.at[me],
            device_id=(me_h, peer), device_id_type=MESH)

    def ends(peer):
        return jnp.logical_or(peer == 0, peer == n_d - 1)

    for j, (step, flip) in enumerate(order):
        peer = peer_at(step, flip)

        @pl.when(jnp.logical_not(ends(peer)))
        def _():
            message(j, peer).start()

    shift_high = pltpu.roll(jnp.concatenate([table_high, jnp.zeros((4, 128 - levels), f32)], axis=1), 1, 1)
    pad_high = jnp.concatenate([table_high, jnp.ones((4, 128 - levels), f32)], axis=1)
    ratio = shift_high / jnp.where(pad_high == 0.0, 1.0, pad_high)
    pad_couple = jnp.concatenate([couple, jnp.ones((4, 128 - levels), f32)], axis=1)
    pivot = pltpu.roll(ratio / pad_couple, 127, 1)
    for k in range(levels - 1):
        wk = column(ratio, k)
        ik = column(pivot, k) if k < levels - 2 else column(last_row, levels - 2)
        for g in range(4):
            wv[k, 8 * g:8 * g + 8, :] = spread(wk, g)
            iv[k, 8 * g:8 * g + 8, :] = spread(ik, g)

    def down(k, carry):
        out = []
        for g in range(4):
            w = wv[k, 8 * g:8 * g + 8, :]
            for q in range(6):
                y = sol[k, q, 8 * g:8 * g + 8, :] + w * carry[g * 6 + q]
                sol[k, q, 8 * g:8 * g + 8, :] = y
                out.append(y)
        return tuple(out)

    start = tuple(sol[0, q, 8 * g:8 * g + 8, :] for g in range(4) for q in range(6))
    lax.fori_loop(1, levels - 1, down, start)

    def rise(i, carry):
        k = levels - 2 - i
        out = []
        for g in range(4):
            piv = iv[k, 8 * g:8 * g + 8, :]
            w = wv[k + 1, 8 * g:8 * g + 8, :]
            for q in range(6):
                x = piv * sol[k, q, 8 * g:8 * g + 8, :] + w * carry[g * 6 + q]
                sol[k, q, 8 * g:8 * g + 8, :] = x
                out.append(x)
        return tuple(out)

    wv[levels - 1] = jnp.zeros((LINES, 128), f32)
    zero = jnp.zeros((8, 128), f32)
    lax.fori_loop(0, levels - 1, rise, (zero,) * 24)
    for q in range(6):
        sol[levels - 1, q] = jnp.zeros((LINES, 128), f32)

    for copy in halo:
        copy.wait()
    third = lax.rem(sub, 3)
    m_first = jnp.where(jnp.logical_and(third == 0, sub < 6), 0.25, 0.0).astype(f32)
    m_third = jnp.where(jnp.logical_and(third == 2, sub < 6), 0.25, 0.0).astype(f32)
    edge_line = (0, LINES - 1)
    for e in range(2):
        sign = 1.0 if e == 0 else -1.0
        line = edge_line[e]
        sum_a = jnp.zeros((8, 128), f32)
        sum_b = jnp.zeros((8, 128), f32)
        for k in range(levels):
            r = 8 + 6 * k
            here = hrecv[e, r:r + 8, :]
            above = hrecv[e, r + 2:r + 10, :] if r + 10 <= 208 else here
            below = hrecv[e, r - 2:r + 6, :]
            d0 = jnp.broadcast_to(dbuf[k, 0, line:line + 1, :], (8, 128))
            d1 = jnp.broadcast_to(dbuf[k, 1, line:line + 1, :], (8, 128))
            d = jnp.where(sub < 3, d0, d1)
            change = d * here + sign * (m_first * above + m_third * below)
            delta[e, k] = change
            hi = jnp.broadcast_to(high[k, line:line + 1, :], (8, 128))
            lo = jnp.broadcast_to(low[k, line:line + 1, :], (8, 128))
            sum_a = sum_a + hi * change
            sum_b = sum_b + lo * change
        p, slot = (0, 0) if e == 0 else (n_d - 1, 1)
        for w, total in enumerate((sum_a, sum_b)):
            for h in range(2):
                rows = pl.ds(p * MSG + row_of(0, w, slot, h), 3, stride=8)
                m1r[rows, :] = m1r[rows, :] + total[3 * h:3 * h + 3, :]
    for j, (step, flip) in enumerate(order):
        peer = peer_at(step, flip)

        @pl.when(ends(peer))
        def _():
            message(j, peer).start()

    r1[me] = m1[me]

    sol2 = sol.reshape(levels * 6 * LINES, 128)
    for e in range(2):
        line = edge_line[e]
        prev = delta[e, 0]
        for k in range(1, levels - 1):
            w = jnp.broadcast_to(wv[k, line:line + 1, :], (8, 128))
            prev = delta[e, k] + w * prev
            delta[e, k] = prev
        x = jnp.zeros((8, 128), f32)
        for k in range(levels - 2, -1, -1):
            piv = jnp.broadcast_to(iv[k, line:line + 1, :], (8, 128))
            x = piv * delta[e, k] + (jnp.broadcast_to(wv[k + 1, line:line + 1, :], (8, 128)) * x if k < levels - 2 else 0.0)
            rows = pl.ds(k * 6 * LINES + line, 6, stride=LINES)
            sol2[rows, :] = sol2[rows, :] + x[0:6, :]

    crecv[me] = cmsg[...]
    for j, (step, flip) in enumerate(order):
        coef_copies[j].wait_send()
    for step, flip in order:
        peer = peer_at(step, flip)
        pltpu.make_async_remote_copy(
            src_ref=cmsg, dst_ref=crecv.at[peer], send_sem=cs_sem.at[0], recv_sem=cr_sem.at[peer],
            device_id=(me_h, peer), device_id_type=MESH).wait_recv()
    o0 = offv[me]
    o1 = offv[me + n_d]
    second = lax.rem(sub // 2, 2) == 1
    alphas, betas, crosses = [], [], []
    for r in range(n_d):
        both = jnp.where(
            second,
            jnp.broadcast_to(crecv[r, pl.ds(o1, 1), :], (8, 128)),
            jnp.broadcast_to(crecv[r, pl.ds(o0, 1), :], (8, 128)))
        alphas.append(jnp.broadcast_to(both[:, 0:1], (8, 128)))
        betas.append(jnp.broadcast_to(both[:, 32:33], (8, 128)))
        crosses.append(jnp.broadcast_to(both[:, 64:65], (8, 128)))
    pivots, steps = [], []
    for r in range(n_d):
        main = 1.0 + alphas[r]
        if r + 1 < n_d:
            main = main + betas[r + 1]
        if r > 0:
            q = crosses[r] * pivots[r - 1]
            steps.append(q)
            main = main - crosses[r] * q
        else:
            steps.append(None)
        pivots.append(1.0 / main)

    for j, (step, flip) in enumerate(order):
        message(j, peer_at(step, flip)).wait_send()
    for step, flip in order:
        peer = peer_at(step, flip)
        pltpu.make_async_remote_copy(
            src_ref=m1.at[0], dst_ref=r1.at[peer], send_sem=s1_sem.at[0], recv_sem=r1_sem.at[peer],
            device_id=(me_h, peer), device_id_type=MESH).wait_recv()
    top = sub < 4
    for f in range(3):
        got = [r1[r, 8 * f:8 * f + 8, :] for r in range(n_d)]
        value = []
        for r in range(n_d):
            t = got[r] + pltpu.roll(got[r + 1], 4, 0) if r + 1 < n_d else got[r]
            t = jnp.where(top, t, pltpu.roll(t, 4, 0))
            if r > 0:
                t = t + steps[r] * value[r - 1]
            value.append(t)
        s = [None] * n_d
        s[n_d - 1] = value[n_d - 1] * pivots[n_d - 1]
        for r in range(n_d - 2, -1, -1):
            s[r] = value[r] * pivots[r] + steps[r + 1] * s[r + 1]
        for r in range(n_d):
            before = s[r - 1] if r > 0 else jnp.zeros((8, 128), f32)
            m2[r, 8 * f:8 * f + 8, :] = jnp.where(top, before, s[r])

    def answer(j, peer):
        return pltpu.make_async_remote_copy(
            src_ref=m2.at[peer], dst_ref=back.at[me], send_sem=s2_sem.at[j], recv_sem=r2_sem.at[me],
            device_id=(me_h, peer), device_id_type=MESH)

    for j, (step, flip) in enumerate(order):
        answer(j, peer_at(step, flip)).start()
    back[me] = m2[me]
    for j, (step, flip) in enumerate(order):
        answer(j, peer_at(step, flip)).wait_send()
    for step, flip in order:
        peer = peer_at(step, flip)
        pltpu.make_async_remote_copy(
            src_ref=m2.at[0], dst_ref=back.at[peer], send_sem=s2_sem.at[0], recv_sem=r2_sem.at[peer],
            device_id=(me_h, peer), device_id_type=MESH).wait_recv()


def write_kernel(n_d, sol, back, low, high, out, stage, ends, sem):
    levels = sol.shape[0]
    per = levels // CHUNKS
    backr = back.reshape(n_d * MSG, 128)
    for g in range(4):
        p0, slot = 8 * (g % 2), g // 2
        for w in range(2):
            for h in range(2):
                for f in range(3):
                    row = p0 * MSG + f * 8 + w * 4 + slot * 2 + h
                    ends[w, h * 3 + f, 8 * g:8 * g + 8, :] = backr[pl.ds(row, 8, stride=MSG), :]

    def copies(c):
        lev = pl.ds(c * per, per)
        return [
            pltpu.make_async_copy(
                stage.at[lev, h * 3 + f], out.at[f, lev, :, pl.ds(h * 128, 128)], sem.at[c, h * 3 + f])
            for h in range(2) for f in range(3)
        ]

    def chunk(c, carry):
        for g in range(4):
            rows = slice(8 * g, 8 * g + 8)
            prev = [ends[0, q, rows, :] for q in range(6)]
            here = [ends[1, q, rows, :] for q in range(6)]
            for l in range(per):
                k = c * per + l
                lo = low[k, rows, :]
                hi = high[k, rows, :]
                for q in range(6):
                    stage[k, q, rows, :] = sol[k, q, rows, :] + (lo * prev[q] + hi * here[q])
        for copy in copies(c):
            copy.start()
        return carry

    lax.fori_loop(0, CHUNKS, chunk, 0)
    for c in range(CHUNKS):
        for copy in copies(c):
            copy.wait()


def body(n_h, n_d, fields, diffusivity, offsets, coupling, inverse):
    f32 = jnp.float32
    levels = fields.shape[1]
    any_spec = pl.BlockSpec(memory_space=pltpu.HBM)
    vmem_spec = pl.BlockSpec(memory_space=pltpu.VMEM)
    V = lambda *shape: pltpu.VMEM(shape, f32)
    dma = lambda *shape: pltpu.SemaphoreType.DMA(shape)
    sol, back, low, high = pl.pallas_call(
        functools.partial(solve_kernel, n_h, n_d),
        out_shape=(
            V(levels, 6, LINES, 128),
            V(n_d, MSG, 128),
            V(levels, LINES, 128),
            V(levels, LINES, 128),
        ),
        in_specs=[any_spec] * 5,
        out_specs=(vmem_spec,) * 4,
        scratch_shapes=[
            V(levels, 6, PAD, 128),
            V(levels, 2, LINES, 128),
            pltpu.SMEM((LINES,), jnp.int32),
            V(4, levels),
            V(4, levels, levels),
            V(levels, LINES, 128),
            V(levels, LINES, 128),
            V(2, 6, LINES, 128),
            V(2, levels, 8, 128),
            V(2, levels * 6, 128),
            V(2, levels * 6 + 16, 128),
            V(8, 128),
            V(n_d, 8, 128),
            V(n_d, MSG, 128),
            V(n_d, MSG, 128),
            V(n_d, MSG, 128),
            dma(CHUNKS, 8),
            dma(3),
            dma(2),
            dma(2),
            dma(n_d),
            dma(n_d),
            dma(n_d),
            dma(n_d),
            dma(n_d),
            dma(n_d),
        ],
        compiler_params=pltpu.CompilerParams(
            collective_id=0, has_side_effects=True, vmem_limit_bytes=48 * 1024 * 1024),
        name="columns",
    )(fields, diffusivity, offsets, coupling, inverse)
    return pl.pallas_call(
        functools.partial(write_kernel, n_d),
        out_shape=jax.ShapeDtypeStruct(fields.shape, f32),
        in_specs=[vmem_spec] * 4,
        out_specs=any_spec,
        scratch_shapes=[
            V(levels, 6, LINES, 128),
            V(2, 6, LINES, 128),
            dma(CHUNKS, 6),
        ],
        compiler_params=pltpu.CompilerParams(vmem_limit_bytes=48 * 1024 * 1024),
        name="assemble",
    )(sol, back, low, high)


def solution(mesh):
    return jax.shard_map(
        functools.partial(body, mesh.shape["horiz"], mesh.shape["depth"]),
        mesh=mesh,
        in_specs=(
            P(None, "depth", "horiz", None),
            P("depth", "horiz", None),
            P("horiz"),
            P(None, "depth"),
            P(None, "depth", None),
        ),
        out_specs=P(None, "depth", "horiz", None),
        check_vma=False,
    )
```

time: 161 us -> 31.7 us (0.20)
  other arithmetic: 64.7 us -> 0 us
  waiting for transfers between devices: 41.9 us -> 0 us
  Pallas kernels: 0 us -> 28.1 us
  local copies, waits for them, and re-layouts: 28.9 us -> 3.4 us
  starting transfers between devices: 19.3 us -> 0 us
  matrix products: 4.28 us -> 0 us
    dynamic_update_slice x32 -> x0, other arithmetic: 52 us -> none  [thomas(): lax.scan(forward_step, (start_ratio, anchor), (lower_band, main_band, upp...]
    all_to_all x1 -> x0, waiting for transfers between devices: 38.6 us -> none  [sent_to_all(): return lax.all_to_all(copies, axis, split_axis=0, concat_axis=0, tiled=True)]
    pallas_call x0 -> x2, Pallas kernels: none -> 28.1 us  [the longest x1 26.1 us: body(): pl.pallas_call(functools.partial(solve_kernel, n_h, n_d), out_shape=(V(le...]
    ppermute x4 -> x0, starting transfers between devices: 10.7 us -> none  [the longest x1 5.75 us: padded_2(): lax.ppermute(lax.slice_in_dim(block, 0, width, axis=dim), axis, backward)]
    all_to_all x1 -> x0, starting transfers between devices: 8.59 us -> none  [sent_to_all(): return lax.all_to_all(copies, axis, split_axis=0, concat_axis=0, tiled=True)]
    slice x5 -> x0, local copies, waits for them, and re-layouts: 7.07 us -> none  [the longest x2 6.18 us: tendency(): north_side = jnp.roll(centre, -1, axis=3)]
    add x3 -> x0, other arithmetic: 6.09 us -> none  [the longest x1 5.3 us: tendency(): pushed = centre + diffusivity[None] * laplace]
    unnamed x22 -> x8, local copies, waits for them, and re-layouts: 9.43 us -> 3.4 us
  transfers between devices with their start and end apart: 5 -> 0, of which waited for: 2 -> 0; matrix products, arithmetic and copies ran while one was open for 16% -> 0% of each run, Pallas kernels for 0% -> 0%
where the time goes in v1:
time: 31.7 us; the launch traced here: 31.5 us
  Pallas kernels  28.1 us (89%)
  local copies, waits for them, and re-layouts  3.4 us (11%)
    pallas_call x1, Pallas kernels, body(): pl.pallas_call(functools.partial(solve_kernel, n_h, n_d), out_shape=(V(le...  26.1 us
    unnamed x8, local copies, waits for them, and re-layouts  3.4 us
    pallas_call x1, Pallas kernels, body(): pl.pallas_call(functools.partial(write_kernel, n_d), out_shape=jax.ShapeD...  2.02 us

profile of v1, /device:TPU:1, one launch (start us, length us, event | category | flops | bytes accessed | tf_op | source)
XLA Modules:
  0.0 31.5 jit_solution(12508084203800190747)
XLA Ops:
  0.0 0.0 copy-start
  0.0 1.2 %copy-done = f32[32,32,256]{2,1,0:T(8,128)S(1)} copy-done((f32[32,32,256]{2,1,0:T(8,128)S(1)}, f32[32,32,256]{2,1,0:T(8,128)}, u32[]{:S(2)}) %copy-start) | copy-done | bytes 1048600
  1.2 0.0 copy-start.1
  1.2 0.8 %copy-done.1 = f32[4,32,32]{2,1,0:T(8,128)S(1)} copy-done((f32[4,32,32]{2,1,0:T(8,128)S(1)}, f32[4,32,32]{2,1,0:T(8,128)}, u32[]{:S(2)}) %copy-start.1) | copy-done | bytes 16408
  2.1 0.0 copy-start.2
  2.1 0.7 %copy-done.2 = f32[4,32]{1,0:T(4,128)S(1)} copy-done((f32[4,32]{1,0:T(4,128)S(1)}, f32[4,32]{1,0:T(4,128)}, u32[]{:S(2)}) %copy-start.2) | copy-done | bytes 536
  2.7 0.0 copy-start.3
  2.8 0.7 %copy-done.3 = s32[32]{0:T(128)S(1)} copy-done((s32[32]{0:T(128)S(1)}, s32[32]{0:T(128)}, u32[]{:S(2)}) %copy-start.3) | copy-done | bytes 152
  3.4 26.1 %columns.1 = (f32[32,6,32,128]{3,2,1,0:T(8,128)S(1)}, f32[16,24,128]{2,1,0:T(8,128)S(1)}, f32[32,32,128]{2,1,0:T(8,128)S(1)}, f32[32,32,128]{2,1,0:T(8,128)S(1)}) custom-call(f32[3,32,32,256]{3,2,1,0:T(8,128)} %fields.1, f32[32,32,256]{2,1,0:T(8,128)S(1)} %copy-done, s32[32]{0:T(128)S(1)} %copy-done.3, f32[4,32]{1,0:T(4,128)S(1)} %copy-done.2, ...), custom_call_target="tpu_custom_call" | custom-call | tf_op jit(solution)/shard_map/columns/pallas_call | solution.py:461
  29.5 2.0 %assemble.1 = f32[3,32,32,256]{3,2,1,0:T(8,128)} custom-call(f32[32,6,32,128]{3,2,1,0:T(8,128)S(1)} %get-tuple-element.9.sol, f32[16,24,128]{2,1,0:T(8,128)S(1)} %get-tuple-element.10.back, f32[32,32,128]{2,1,0:T(8,128)S(1)} %get-tuple-element.11.low, f32[32,32,128]{2,1,0:T(8,128)S(1)} %get-tuple-element.12.high), custom_call_target="tpu_custom_call" | custom-call | tf_op jit(solution)/shard_map/assemble/pallas_call | solution.py:503
Async XLA Ops:
  0.0 1.2 %copy-start = (f32[32,32,256]{2,1,0:T(8,128)S(1)}, f32[32,32,256]{2,1,0:T(8,128)}, u32[]{:S(2)}) copy-start(f32[32,32,256]{2,1,0:T(8,128)} %diff.1) | copy-start | bytes 3145732
  1.2 0.8 %copy-start.1 = (f32[4,32,32]{2,1,0:T(8,128)S(1)}, f32[4,32,32]{2,1,0:T(8,128)}, u32[]{:S(2)}) copy-start(f32[4,32,32]{2,1,0:T(8,128)} %inv.1) | copy-start | bytes 49156
  2.1 0.7 %copy-start.2 = (f32[4,32]{1,0:T(4,128)S(1)}, f32[4,32]{1,0:T(4,128)}, u32[]{:S(2)}) copy-start(f32[4,32]{1,0:T(4,128)} %coup.1) | copy-start | bytes 1540
  2.7 0.7 %copy-start.3 = (s32[32]{0:T(128)S(1)}, s32[32]{0:T(128)}, u32[]{:S(2)}) copy-start(s32[32]{0:T(128)} %offs.1) | copy-start | bytes 388

commit v2 on v1

v2 whole, which is shorter than its diff:
```python
import functools

import jax
import jax.numpy as jnp
from jax import lax
from jax.experimental import pallas as pl
from jax.experimental.pallas import tpu as pltpu
from jax.sharding import PartitionSpec as P

MESH = pl.DeviceIdType.MESH
CHUNKS = 4
PAD = 48
LINES = 32
GROUPS = LINES // 8
UNITS = GROUPS * 6
HALF = UNITS // 2


def depth_order(n):
    half = n // 2
    steps = sorted(range(half), key=lambda s: -min(s, half - s))
    return [(s, c) for s in steps for c in (0, 1) if (s, c) != (0, 0)]


def columns_kernel(
    n_h, n_d,
    fields, diff, offs, coup, inv,
    sol, back, low, high,
    fbuf, dbuf, offv, cvec, kvec, offl, wv, iv, delta,
    hsend, hrecv, cmsg, crecv, m1, r1, m2, em, er, comp, ucoef,
    edge_sem, load_sem, small_sem, hs_sem, hr_sem, cs_sem, cr_sem, s1_sem, r1_sem, s2_sem, r2_sem,
    es_sem, er_sem,
):
    f32 = jnp.float32
    levels = fields.shape[1]
    per = levels // CHUNKS
    me_h = lax.axis_index("horiz")
    me = lax.axis_index("depth")
    east = lax.rem(me_h + 1, n_h)
    west = lax.rem(me_h + n_h - 1, n_h)
    z, core = me // 2, lax.rem(me, 2)
    order = depth_order(n_d)
    quads = n_d // 4

    def peer_at(step, flip):
        return lax.rem(z + step, n_d // 2) * 2 + (core if flip == 0 else 1 - core)

    def to_depth(peer):
        return (me_h, peer)

    def remote(src, dst, send, recv, to):
        return pltpu.make_async_remote_copy(
            src_ref=src, dst_ref=dst, send_sem=send, recv_sem=recv, device_id=to, device_id_type=MESH)

    barrier = pltpu.get_barrier_semaphore()
    for to in (east, west):
        pl.semaphore_signal(barrier, inc=1, device_id=(to, me), device_id_type=MESH)
    for step, flip in order:
        pl.semaphore_signal(barrier, inc=1, device_id=to_depth(peer_at(step, flip)), device_id_type=MESH)

    small = [
        pltpu.make_async_copy(offs, offv, small_sem.at[0]),
        pltpu.make_async_copy(coup, cvec, small_sem.at[1]),
        pltpu.make_async_copy(inv, kvec, small_sem.at[2]),
    ]
    outer = []
    for i, first in enumerate((0, LINES - 8)):
        for h in range(2):
            for f in range(3):
                outer.append(pltpu.make_async_copy(
                    fields.at[f, :, pl.ds(first, 8), pl.ds(h * 128, 128)],
                    fbuf.at[:, h * 3 + f, pl.ds(8 + first, 8), :],
                    edge_sem.at[i, h * 3 + f]))

    def chunk_copies(c):
        lev = pl.ds(c * per, per)
        out = []
        for h in range(2):
            lane = pl.ds(h * 128, 128)
            for f in range(3):
                out.append(pltpu.make_async_copy(
                    fields.at[f, lev, pl.ds(8, LINES - 16), lane],
                    fbuf.at[lev, h * 3 + f, pl.ds(16, LINES - 16), :],
                    load_sem.at[c, h * 3 + f]))
            out.append(pltpu.make_async_copy(
                diff.at[lev, :, lane], dbuf.at[lev, h], load_sem.at[c, 6 + h]))
        return out

    for copy in small + outer:
        copy.start()
    for c in range(CHUNKS):
        for copy in chunk_copies(c):
            copy.start()

    f2 = fbuf.reshape(levels * 6 * PAD, 128)
    f2[pl.ds(7, levels * 6, stride=PAD), :] = jnp.zeros((levels * 6, 128), f32)
    f2[pl.ds(40, levels * 6, stride=PAD), :] = jnp.zeros((levels * 6, 128), f32)
    for e in range(2):
        hrecv[e, 0:8, :] = jnp.zeros((8, 128), f32)
        hrecv[e, 200:208, :] = jnp.zeros((8, 128), f32)
    m1[...] = jnp.zeros(m1.shape, f32)

    for copy in small:
        copy.wait()
    sub = lax.broadcasted_iota(jnp.int32, (8, 128), 0)
    lane = lax.broadcasted_iota(jnp.int32, (8, 128), 1)
    masks = []
    for g in range(GROUPS):
        v = jnp.full((8, 128), offv[8 * g], jnp.int32)
        for i in range(1, 8):
            v = jnp.where(sub == i, offv[8 * g + i], v)
        offl[g] = v
        masks.append([v == o for o in range(3)])

    def widen(x):
        return jnp.concatenate([x, jnp.zeros((4, 128 - levels), f32)], axis=1)

    couple = cvec[...]
    first_row = kvec[:, 0, :]
    last_row = kvec[:, levels - 2, :]
    c_low = couple[:, 0:1]
    c_high = couple[:, levels - 1:levels]
    gate = jnp.where(me > 0, 1.0, 0.0).astype(f32)
    table_low = first_row * (jnp.broadcast_to(c_low, (4, levels)) * gate)
    table_high = last_row * jnp.broadcast_to(c_high, (4, levels))
    lane4 = lax.broadcasted_iota(jnp.int32, (4, 128), 1)

    def pick(rows, m):
        return jnp.where(m[0], rows[0], jnp.where(m[1], rows[1], jnp.where(m[2], rows[2], rows[3])))

    def by_line(table):
        rows = [jnp.broadcast_to(table[o:o + 1, :], (8, 128)) for o in range(4)]
        return [pick(rows, masks[g]) for g in range(GROUPS)]

    def fill(ref, table, count):
        lines = by_line(table)
        for k in range(count):
            for g in range(GROUPS):
                ref[k, 8 * g:8 * g + 8, :] = jnp.broadcast_to(lines[g][:, k:k + 1], (8, 128))

    wide_high = widen(table_high)
    fill(low, jnp.where(lane4 == levels - 1, 0.0, widen(table_low)), levels)
    fill(high, jnp.where(lane4 == levels - 1, 1.0, wide_high), levels)

    c_low4 = jnp.broadcast_to(c_low, (4, 128))
    c_high4 = jnp.broadcast_to(c_high, (4, 128))
    alpha = c_high4 - c_high4 * jnp.broadcast_to(table_high[:, levels - 2:levels - 1], (4, 128))
    beta = c_low4 - c_low4 * jnp.broadcast_to(table_low[:, 0:1], (4, 128))
    cross = c_high4 * jnp.broadcast_to(table_low[:, levels - 2:levels - 1], (4, 128))
    packed = jnp.where(lane4 < 32, alpha, jnp.where(lane4 < 64, beta, cross))
    cmsg[0:4, :] = packed
    cmsg[4:8, :] = packed

    for copy in outer:
        copy.wait()
    hsend[0] = f2[pl.ds(39, levels * 6, stride=PAD), :]
    hsend[1] = f2[pl.ds(8, levels * 6, stride=PAD), :]
    pl.semaphore_wait(barrier, 2 + len(order))
    halo = [
        remote(hsend.at[e], hrecv.at[e, pl.ds(8, levels * 6), :], hs_sem.at[e], hr_sem.at[e], (to, me))
        for e, to in ((0, east), (1, west))
    ]
    for copy in halo:
        copy.start()

    def coef_copy(j, peer):
        return remote(cmsg, crecv.at[me], cs_sem.at[j], cr_sem.at[me], to_depth(peer))

    for j, (step, flip) in enumerate(order):
        coef_copy(j, peer_at(step, flip)).start()

    is_last = lane == 127
    is_first = lane == 0

    def forcing(c, g):
        r0 = 8 + 8 * g
        rows = slice(8 * g, 8 * g + 8)
        sums = [m1[g * 6 + q, 8 * w:8 * w + 8, :] for w in range(2) for q in range(6)]
        for l in range(per):
            k = c * per + l
            hi = high[k, rows, :]
            lo = low[k, rows, :]
            mid = [fbuf[k, q, r0:r0 + 8, :] for q in range(6)]
            es = [fbuf[k, q, r0 + 1:r0 + 9, :] for q in range(6)]
            ws = [fbuf[k, q, r0 - 1:r0 + 7, :] for q in range(6)]
            up = [pltpu.roll(mid[q], 127, 1) for q in range(6)]
            dn = [pltpu.roll(mid[q], 1, 1) for q in range(6)]
            for h in range(2):
                d = dbuf[k, h, rows, :]
                keep = 1.0 - 4.0 * d
                q = [h * 3 + f for f in range(3)]
                qo = [(1 - h) * 3 + f for f in range(3)]
                north = [jnp.where(is_last, up[qo[f]], up[q[f]]) for f in range(3)]
                south = [jnp.where(is_first, dn[qo[f]], dn[q[f]]) for f in range(3)]
                base = [
                    mid[q[f]] * keep + d * ((es[q[f]] + ws[q[f]]) + (north[f] + south[f]))
                    for f in range(3)
                ]
                out = [
                    base[0] - 0.25 * (es[q[2]] - ws[q[2]]),
                    base[1] - 0.25 * (north[2] - south[2]),
                    base[2] - 0.25 * ((es[q[0]] - ws[q[0]]) + (north[1] - south[1])),
                ]
                for f in range(3):
                    sol[k, q[f], rows, :] = out[f]
                    sums[q[f]] = sums[q[f]] + hi * out[f]
                    sums[6 + q[f]] = sums[6 + q[f]] + lo * out[f]
        for w in range(2):
            for q in range(6):
                m1[g * 6 + q, 8 * w:8 * w + 8, :] = sums[w * 6 + q]

    def solver_of(slot, quad, m):
        return quad * 4 + m + slot, slot * HALF + quad * 3 + m

    def targets(slot):
        for i, dq in enumerate((2, 1, 3, 0)):
            quad = lax.rem(me // 4 + dq, quads)
            for m in range(3):
                peer, unit = solver_of(slot, quad, m)
                yield slot * HALF + i * 3 + m, peer, unit

    def target_copy(slot, j, peer, unit):
        return remote(m1.at[unit], r1.at[slot, me], s1_sem.at[j], r1_sem.at[slot, me], to_depth(peer))

    for slot in range(2):
        def step_chunk(c, carry):
            if slot == 0:
                for copy in chunk_copies(c):
                    copy.wait()
            for g in range(2 * slot, 2 * slot + 2):
                forcing(c, g)
            return carry

        lax.fori_loop(0, CHUNKS, step_chunk, 0)
        for j, peer, unit in targets(slot):
            @pl.when(peer != me)
            def _():
                target_copy(slot, j, peer, unit).start()

            @pl.when(peer == me)
            def _():
                r1[slot, me] = m1[unit]

    shift_high = pltpu.roll(wide_high, 1, 1)
    inner = jnp.logical_and(lane4 > 0, lane4 < levels - 1)
    ratio = jnp.where(inner, shift_high / jnp.where(inner, wide_high, 1.0), 0.0)
    inner_c = jnp.where(inner, widen(couple), 1.0)
    pivot = pltpu.roll(ratio / inner_c, 127, 1)
    pivot = jnp.where(lane4 == levels - 2, widen(last_row), pivot)
    fill(wv, ratio, levels)
    fill(iv, pivot, levels - 1)

    def down(k, carry):
        out = []
        for g in range(GROUPS):
            rows = slice(8 * g, 8 * g + 8)
            w = wv[k, rows, :]
            for q in range(6):
                y = sol[k, q, rows, :] + w * carry[g * 6 + q]
                sol[k, q, rows, :] = y
                out.append(y)
        return tuple(out)

    def rise(i, carry):
        k = levels - 2 - i
        out = []
        for g in range(GROUPS):
            rows = slice(8 * g, 8 * g + 8)
            piv = iv[k, rows, :]
            w = wv[k + 1, rows, :]
            for q in range(6):
                x = piv * sol[k, q, rows, :] + w * carry[g * 6 + q]
                sol[k, q, rows, :] = x
                out.append(x)
        return tuple(out)

    zero = jnp.zeros((8, 128), f32)
    lax.fori_loop(1, levels - 1, down,
                  tuple(sol[0, q, 8 * g:8 * g + 8, :] for g in range(GROUPS) for q in range(6)))
    lax.fori_loop(0, levels - 1, rise, (zero,) * UNITS)
    for q in range(6):
        sol[levels - 1, q] = jnp.zeros((LINES, 128), f32)

    crecv[me] = cmsg[...]
    for step, flip in order:
        peer = peer_at(step, flip)
        remote(cmsg, crecv.at[peer], cs_sem.at[0], cr_sem.at[peer], to_depth(peer)).wait_recv()
    alphas, betas, crosses = [], [], []
    for r in range(n_d):
        tile = crecv[r]
        alphas.append(jnp.broadcast_to(tile[:, 0:1], (8, 128)))
        betas.append(jnp.broadcast_to(tile[:, 32:33], (8, 128)))
        crosses.append(jnp.broadcast_to(tile[:, 64:65], (8, 128)))
    mains = [1.0 + alphas[r] + (betas[r + 1] if r + 1 < n_d else 0.0) for r in range(n_d)]
    before = None
    for r in range(n_d):
        q = crosses[r] * before if r > 0 else zero
        main = mains[r] - crosses[r] * q if r > 0 else mains[r]
        before = 1.0 / main
        comp[0, r] = q
        comp[1, r] = before
        comp[4, r] = crosses[r]
    after = None
    for r in range(n_d - 1, -1, -1):
        q = crosses[r + 1] * after if r + 1 < n_d else zero
        main = mains[r] - crosses[r + 1] * q if r + 1 < n_d else mains[r]
        after = 1.0 / main
        comp[2, r] = q
        comp[3, r] = main

    for copy in halo:
        copy.wait_recv()
    third = lax.rem(sub, 3)
    m_first = jnp.where(jnp.logical_and(third == 0, sub < 6), 0.25, 0.0).astype(f32)
    m_third = jnp.where(jnp.logical_and(third == 2, sub < 6), 0.25, 0.0).astype(f32)
    edge_line = (0, LINES - 1)
    edge_off = [offv[0], offv[LINES - 1]]
    me_low = jnp.maximum(me - 1, 0)

    def one(ref, line):
        return jnp.broadcast_to(ref[line:line + 1, :], (8, 128))

    def edge_comp(i, r, e):
        return jnp.broadcast_to(comp[i, r, pl.ds(edge_off[e], 1), :], (8, 128))

    edge_sums = []
    for e in range(2):
        sign = 1.0 if e == 0 else -1.0
        line = edge_line[e]
        sum_a = [zero, zero]
        sum_b = [zero, zero]
        for k in range(levels):
            r = 8 + 6 * k
            here = hrecv[e, r:r + 8, :]
            above = hrecv[e, r + 2:r + 10, :]
            below = hrecv[e, r - 2:r + 6, :]
            d = jnp.where(sub < 3, one(dbuf.at[k, 0], line), one(dbuf.at[k, 1], line))
            change = d * here + sign * (m_first * above + m_third * below)
            delta[e, k] = change
            sum_a[k % 2] = sum_a[k % 2] + one(high.at[k], line) * change
            sum_b[k % 2] = sum_b[k % 2] + one(low.at[k], line) * change
        sum_a = sum_a[0] + sum_a[1]
        sum_b = sum_b[0] + sum_b[1]
        edge_sums.append((sum_a, sum_b))
        em[0, 8 * e:8 * e + 8, :] = sum_a + edge_comp(0, me, e) * sum_b
        em[1, 8 * e:8 * e + 8, :] = sum_b + edge_comp(2, me_low, e) * sum_a

    def edge_copy(j, peer):
        side = jnp.where(peer > me, 0, 1)
        return remote(em.at[side], er.at[me], es_sem.at[j], er_sem.at[me], to_depth(peer))

    for j, (step, flip) in enumerate(order):
        edge_copy(j, peer_at(step, flip)).start()

    quad, place = me // 4, lax.rem(me, 4)
    has = [place != 3, place != 0]
    units = [quad * 3 + jnp.minimum(place, 2), HALF + quad * 3 + jnp.maximum(place - 1, 0)]

    for slot in range(2):
        @pl.when(has[slot])
        def _():
            v = offl[units[slot] // 6]
            m = [v == o for o in range(3)]
            for i in range(2):
                for r in range(n_d):
                    ucoef[slot, i, r] = pick([one(comp.at[i, r], o) for o in range(4)], m)

    def answer(slot, j, peer):
        return remote(m2.at[slot, peer], back.at[units[slot]], s2_sem.at[slot, j],
                      r2_sem.at[units[slot]], to_depth(peer))

    for slot in range(2):
        @pl.when(has[slot])
        def _():
            for step, flip in order:
                peer = peer_at(step, flip)
                remote(m1.at[0], r1.at[slot, peer], s1_sem.at[0], r1_sem.at[slot, peer],
                       to_depth(peer)).wait_recv()
            value = None
            values = []
            for r in range(n_d):
                t = r1[slot, r, 0:8, :]
                if r + 1 < n_d:
                    t = t + r1[slot, r + 1, 8:16, :]
                value = t if r == 0 else t + ucoef[slot, 0, r] * value
                values.append(value)
            s = values[n_d - 1] * ucoef[slot, 1, n_d - 1]
            for r in range(n_d - 1, -1, -1):
                m2[slot, r, 8:16, :] = s
                if r + 1 < n_d:
                    m2[slot, r + 1, 0:8, :] = s
                if r > 0:
                    s = values[r - 1] * ucoef[slot, 1, r - 1] + ucoef[slot, 0, r] * s
            m2[slot, 0, 0:8, :] = zero
            for j, (step, flip) in enumerate(order):
                answer(slot, j, peer_at(step, flip)).start()
            back[units[slot]] = m2[slot, me]

    sol2 = sol.reshape(levels * 6 * LINES, 128)
    for e in range(2):
        line = edge_line[e]
        prev = delta[e, 0]
        for k in range(1, levels - 1):
            prev = delta[e, k] + one(wv.at[k], line) * prev
            delta[e, k] = prev
        x = zero
        for k in range(levels - 2, -1, -1):
            x = one(iv.at[k], line) * delta[e, k] + one(wv.at[k + 1], line) * x
            rows = pl.ds(k * 6 * LINES + line, 6, stride=LINES)
            sol2[rows, :] = sol2[rows, :] + x[0:6, :]

    for step, flip in order:
        peer = peer_at(step, flip)
        remote(em.at[0], er.at[peer], es_sem.at[0], er_sem.at[peer], to_depth(peer)).wait_recv()
    edge_values = []
    for e in range(2):
        v = zero
        w = zero
        rows = slice(8 * e, 8 * e + 8)
        for r in range(n_d):
            v = jnp.where(r < me, er[r, rows, :] + edge_comp(0, r, e) * v, v)
        for r in range(n_d - 1, 0, -1):
            w = jnp.where(r > me, er[r, rows, :] + edge_comp(2, r - 1, e) * w, w)
        v = v + edge_sums[e][1]
        w = w + edge_sums[e][0]
        q_me = edge_comp(0, me, e)
        u_me = edge_comp(4, me, e)
        s_here = (w + q_me * v) / (edge_comp(3, me, e) - u_me * q_me)
        s_before = (v + u_me * s_here) * edge_comp(1, me_low, e)
        edge_values.append((jnp.where(me > 0, s_before, 0.0), s_here))

    for slot in range(2):
        for unit in range(slot * HALF, (slot + 1) * HALF):
            i = unit - slot * HALF
            peer, _ = solver_of(slot, i // 3, i % 3)

            @pl.when(me != peer)
            def _():
                remote(m2.at[slot, 0], back.at[unit], s2_sem.at[slot, 0], r2_sem.at[unit],
                       to_depth(peer)).wait_recv()
    back2 = back.reshape((UNITS + 2) * 16, 128)
    for e in range(2):
        unit0 = 0 if e == 0 else UNITS - 6
        for w in range(2):
            rows = pl.ds(unit0 * 16 + 8 * w + 7 * e, 6, stride=16)
            back2[rows, :] = back2[rows, :] + edge_values[e][w][0:6, :]
    for copy in halo:
        copy.wait_send()
    for j, (step, flip) in enumerate(order):
        peer = peer_at(step, flip)
        coef_copy(j, peer).wait_send()
        edge_copy(j, peer).wait_send()
    for slot in range(2):
        for j, peer, unit in targets(slot):
            @pl.when(peer != me)
            def _():
                target_copy(slot, j, peer, unit).wait_send()

        @pl.when(has[slot])
        def _():
            for j, (step, flip) in enumerate(order):
                answer(slot, j, peer_at(step, flip)).wait_send()


def assemble_kernel(sol, back, low, high, out, stage, sem):
    levels = sol.shape[0]
    per = levels // CHUNKS

    def copies(c):
        lev = pl.ds(c * per, per)
        return [
            pltpu.make_async_copy(
                stage.at[lev, h * 3 + f], out.at[f, lev, :, pl.ds(h * 128, 128)], sem.at[c, h * 3 + f])
            for h in range(2) for f in range(3)
        ]

    def chunk(c, carry):
        for g in range(GROUPS):
            rows = slice(8 * g, 8 * g + 8)
            prev = [back[g * 6 + q, 0:8, :] for q in range(6)]
            here = [back[g * 6 + q, 8:16, :] for q in range(6)]
            for l in range(per):
                k = c * per + l
                lo = low[k, rows, :]
                hi = high[k, rows, :]
                for q in range(6):
                    stage[k, q, rows, :] = sol[k, q, rows, :] + (lo * prev[q] + hi * here[q])
        for copy in copies(c):
            copy.start()
        return carry

    lax.fori_loop(0, CHUNKS, chunk, 0)
    for c in range(CHUNKS):
        for copy in copies(c):
            copy.wait()


def body(n_h, n_d, fields, diffusivity, offsets, coupling, inverse):
    f32 = jnp.float32
    levels = fields.shape[1]
    hbm_spec = pl.BlockSpec(memory_space=pltpu.HBM)
    vmem_spec = pl.BlockSpec(memory_space=pltpu.VMEM)
    V = lambda *shape: pltpu.VMEM(shape, f32)
    dma = lambda *shape: pltpu.SemaphoreType.DMA(shape)
    sol, back, low, high = pl.pallas_call(
        functools.partial(columns_kernel, n_h, n_d),
        out_shape=(
            V(levels, 6, LINES, 128),
            V(UNITS + 2, 16, 128),
            V(levels, LINES, 128),
            V(levels, LINES, 128),
        ),
        in_specs=[hbm_spec] * 5,
        out_specs=(vmem_spec,) * 4,
        scratch_shapes=[
            V(levels, 6, PAD, 128),
            V(levels, 2, LINES, 128),
            pltpu.SMEM((LINES,), jnp.int32),
            V(4, levels),
            V(4, levels, levels),
            pltpu.VMEM((GROUPS, 8, 128), jnp.int32),
            V(levels, LINES, 128),
            V(levels, LINES, 128),
            V(2, levels, 8, 128),
            V(2, levels * 6, 128),
            V(2, levels * 6 + 16, 128),
            V(8, 128),
            V(n_d, 8, 128),
            V(UNITS, 16, 128),
            V(2, n_d, 16, 128),
            V(2, n_d, 16, 128),
            V(2, 16, 128),
            V(n_d, 16, 128),
            V(5, n_d, 8, 128),
            V(2, 2, n_d, 8, 128),
            dma(2, 6),
            dma(CHUNKS, 8),
            dma(3),
            dma(2),
            dma(2),
            dma(n_d),
            dma(n_d),
            dma(UNITS),
            dma(2, n_d),
            dma(2, n_d),
            dma(UNITS),
            dma(n_d),
            dma(n_d),
        ],
        compiler_params=pltpu.CompilerParams(
            collective_id=0, has_side_effects=True, vmem_limit_bytes=48 * 1024 * 1024),
        name="columns",
    )(*(pltpu.with_memory_space_constraint(x, pltpu.HBM)
        for x in (fields, diffusivity, offsets, coupling, inverse)))
    return pl.pallas_call(
        assemble_kernel,
        out_shape=jax.ShapeDtypeStruct(fields.shape, f32),
        in_specs=[vmem_spec] * 4,
        out_specs=hbm_spec,
        scratch_shapes=[
            V(levels, 6, LINES, 128),
            dma(CHUNKS, 6),
        ],
        compiler_params=pltpu.CompilerParams(vmem_limit_bytes=48 * 1024 * 1024),
        name="assemble",
    )(sol, back, low, high)


def solution(mesh):
    return jax.shard_map(
        functools.partial(body, mesh.shape["horiz"], mesh.shape["depth"]),
        mesh=mesh,
        in_specs=(
            P(None, "depth", "horiz", None),
            P("depth", "horiz", None),
            P("horiz"),
            P(None, "depth"),
            P(None, "depth", None),
        ),
        out_specs=P(None, "depth", "horiz", None),
        check_vma=False,
    )
```

time: 31.7 us -> 29.8 us (0.940)
  local copies, waits for them, and re-layouts: 3.4 us -> 0 us
  Pallas kernels: 28.1 us -> 29.7 us
    unnamed x8 -> x0, local copies, waits for them, and re-layouts: 3.4 us -> none
    pallas_call x2, Pallas kernels: 28.1 us -> 29.7 us  [the longest x1 27.7 us: body(): pl.pallas_call(functools.partial(columns_kernel, n_h, n_d), out_shape=(V(...]
where the time goes in v2:
time: 29.8 us; the launch traced here: 29.7 us
  Pallas kernels  29.7 us (100%)
    pallas_call x1, Pallas kernels, body(): pl.pallas_call(functools.partial(columns_kernel, n_h, n_d), out_shape=(V(...  27.7 us
    pallas_call x1, Pallas kernels, body(): pl.pallas_call(assemble_kernel, out_shape=jax.ShapeDtypeStruct(fields.sha...  1.98 us

profile of v2, /device:TPU:1, one launch (start us, length us, event | category | flops | bytes accessed | tf_op | source)
XLA Modules:
  0.0 29.7 jit_solution(7848525664095556566)
XLA Ops:
  0.0 27.7 %columns.1 = (f32[32,6,32,128]{3,2,1,0:T(8,128)S(1)}, f32[26,16,128]{2,1,0:T(8,128)S(1)}, f32[32,32,128]{2,1,0:T(8,128)S(1)}, f32[32,32,128]{2,1,0:T(8,128)S(1)}) custom-call(f32[3,32,32,256]{3,2,1,0:T(8,128)} %fields.1, f32[32,32,256]{2,1,0:T(8,128)} %diff.1, s32[32]{0:T(128)} %offs.1, f32[4,32]{1,0:T(4,128)} %coup.1, f32[4,32,32]{2,1,0:T(8,128)} %inv.1), custom_call_target="tpu_custom_call" | custom-call | tf_op jit(solution)/shard_map/columns/pallas_call | solution.py:505
  27.8 2.0 %assemble.1 = f32[3,32,32,256]{3,2,1,0:T(8,128)} custom-call(f32[32,6,32,128]{3,2,1,0:T(8,128)S(1)} %get-tuple-element.9.sol, f32[26,16,128]{2,1,0:T(8,128)S(1)} %get-tuple-element.10.back, f32[32,32,128]{2,1,0:T(8,128)S(1)} %get-tuple-element.11.low, f32[32,32,128]{2,1,0:T(8,128)S(1)} %get-tuple-element.12.high), custom_call_target="tpu_custom_call" | custom-call | tf_op jit(solution)/shard_map/assemble/pallas_call | solution.py:555

commit v3 on v2

--- a/solution.py
+++ b/solution.py
@@ -16,10 +16,8 @@
 HALF = UNITS // 2
 
 
-def depth_order(n):
-    half = n // 2
-    steps = sorted(range(half), key=lambda s: -min(s, half - s))
-    return [(s, c) for s in steps for c in (0, 1) if (s, c) != (0, 0)]
+def far_first(chips):
+    return sorted(range(1, chips), key=lambda s: -min(s, chips - s))
 
 
 def columns_kernel(
@@ -27,9 +25,10 @@
     fields, diff, offs, coup, inv,
     sol, back, low, high,
     fbuf, dbuf, offv, cvec, kvec, offl, wv, iv, delta,
-    hsend, hrecv, cmsg, crecv, m1, r1, m2, em, er, comp, ucoef,
-    edge_sem, load_sem, small_sem, hs_sem, hr_sem, cs_sem, cr_sem, s1_sem, r1_sem, s2_sem, r2_sem,
-    es_sem, er_sem,
+    hsend, hrecv, cmsg, cpart, chip, crecv, m1, other, chip_rows, middle, r1, m2, got, pass_on,
+    esum, epart, em, er, comp, ucoef, lcoef,
+    edge_sem, load_sem, small_sem, hs_sem, hr_sem, pair_send, pair_recv, cs_sem, cr_sem,
+    s1_sem, r1_sem, s2_sem, r2_sem, es_sem, er_sem,
 ):
     f32 = jnp.float32
     levels = fields.shape[1]
@@ -39,24 +38,26 @@
     east = lax.rem(me_h + 1, n_h)
     west = lax.rem(me_h + n_h - 1, n_h)
     z, core = me // 2, lax.rem(me, 2)
-    order = depth_order(n_d)
-    quads = n_d // 4
-
-    def peer_at(step, flip):
-        return lax.rem(z + step, n_d // 2) * 2 + (core if flip == 0 else 1 - core)
-
-    def to_depth(peer):
-        return (me_h, peer)
+    chips = n_d // 2
+    steps = far_first(chips)
+    on_low = core == 0
+
+    def chip_at(step):
+        return lax.rem(z + step, chips)
+
+    def same_core(zz):
+        return (me_h, zz * 2 + core)
+
+    partner = (me_h, z * 2 + 1 - core)
 
     def remote(src, dst, send, recv, to):
         return pltpu.make_async_remote_copy(
             src_ref=src, dst_ref=dst, send_sem=send, recv_sem=recv, device_id=to, device_id_type=MESH)
 
     barrier = pltpu.get_barrier_semaphore()
-    for to in (east, west):
-        pl.semaphore_signal(barrier, inc=1, device_id=(to, me), device_id_type=MESH)
-    for step, flip in order:
-        pl.semaphore_signal(barrier, inc=1, device_id=to_depth(peer_at(step, flip)), device_id_type=MESH)
+    meets = [(east, me), (west, me), partner] + [same_core(chip_at(step)) for step in steps]
+    for to in meets:
+        pl.semaphore_signal(barrier, inc=1, device_id=to, device_id_type=MESH)
 
     small = [
         pltpu.make_async_copy(offs, offv, small_sem.at[0]),
@@ -155,20 +156,6 @@
         copy.wait()
     hsend[0] = f2[pl.ds(39, levels * 6, stride=PAD), :]
     hsend[1] = f2[pl.ds(8, levels * 6, stride=PAD), :]
-    pl.semaphore_wait(barrier, 2 + len(order))
-    halo = [
-        remote(hsend.at[e], hrecv.at[e, pl.ds(8, levels * 6), :], hs_sem.at[e], hr_sem.at[e], (to, me))
-        for e, to in ((0, east), (1, west))
-    ]
-    for copy in halo:
-        copy.start()
-
-    def coef_copy(j, peer):
-        return remote(cmsg, crecv.at[me], cs_sem.at[j], cr_sem.at[me], to_depth(peer))
-
-    for j, (step, flip) in enumerate(order):
-        coef_copy(j, peer_at(step, flip)).start()
-
     is_last = lane == 127
     is_first = lane == 0
 
@@ -209,22 +196,9 @@
             for q in range(6):
                 m1[g * 6 + q, 8 * w:8 * w + 8, :] = sums[w * 6 + q]
 
-    def solver_of(slot, quad, m):
-        return quad * 4 + m + slot, slot * HALF + quad * 3 + m
-
-    def targets(slot):
-        for i, dq in enumerate((2, 1, 3, 0)):
-            quad = lax.rem(me // 4 + dq, quads)
-            for m in range(3):
-                peer, unit = solver_of(slot, quad, m)
-                yield slot * HALF + i * 3 + m, peer, unit
-
-    def target_copy(slot, j, peer, unit):
-        return remote(m1.at[unit], r1.at[slot, me], s1_sem.at[j], r1_sem.at[slot, me], to_depth(peer))
-
-    for slot in range(2):
+    def slot_forcing(slot, first):
         def step_chunk(c, carry):
-            if slot == 0:
+            if first:
                 for copy in chunk_copies(c):
                     copy.wait()
             for g in range(2 * slot, 2 * slot + 2):
@@ -232,14 +206,95 @@
             return carry
 
         lax.fori_loop(0, CHUNKS, step_chunk, 0)
-        for j, peer, unit in targets(slot):
-            @pl.when(peer != me)
-            def _():
-                target_copy(slot, j, peer, unit).start()
-
-            @pl.when(peer == me)
-            def _():
-                r1[slot, me] = m1[unit]
+
+    for slot in range(2):
+        @pl.when(core == 1 - slot)
+        def _():
+            slot_forcing(slot, True)
+
+    halo = [
+        remote(hsend.at[e], hrecv.at[e, pl.ds(8, levels * 6), :], hs_sem.at[e], hr_sem.at[e], (to, me))
+        for e, to in ((0, east), (1, west))
+    ]
+    pair_coef = remote(cmsg, cpart, pair_send.at[0], pair_recv.at[0], partner)
+    pair_rows = remote(m1.at[pl.ds((1 - core) * HALF, HALF)], other, pair_send.at[1], pair_recv.at[1], partner)
+    pl.semaphore_wait(barrier, len(meets))
+    for copy in (pair_coef, pair_rows, *halo):
+        copy.start()
+    for slot in range(2):
+        @pl.when(core == slot)
+        def _():
+            slot_forcing(slot, False)
+
+    def splat(tile, at):
+        return jnp.broadcast_to(tile[:, at:at + 1], (8, 128))
+
+    pair_coef.wait_recv()
+    mine, theirs = cmsg[...], cpart[...]
+    tile0 = jnp.where(on_low, mine, theirs)
+    tile1 = jnp.where(on_low, theirs, mine)
+    alpha0, beta0, cross0 = (splat(tile0, at) for at in (0, 32, 64))
+    alpha1, beta1, cross1 = (splat(tile1, at) for at in (0, 32, 64))
+    mid_pivot = 1.0 / (1.0 + alpha0 + beta1)
+    to_low = cross0 * mid_pivot
+    to_high = cross1 * mid_pivot
+    chip[...] = jnp.where(
+        lane < 32, alpha1 - cross1 * to_high,
+        jnp.where(lane < 64, beta0 - cross0 * to_low, cross0 * to_high))
+    lcoef[0] = to_low
+    lcoef[1] = to_high
+    lcoef[2] = mid_pivot
+
+    def coef_copy(j, zz):
+        return remote(chip, crecv.at[z], cs_sem.at[j], cr_sem.at[z], same_core(zz))
+
+    for j, step in enumerate(steps):
+        coef_copy(j, chip_at(step)).start()
+
+    def one(ref, line):
+        return jnp.broadcast_to(ref[line:line + 1, :], (8, 128))
+
+    def group_masks(g):
+        v = offl[g]
+        return [v == o for o in range(3)]
+
+    own_masks = [group_masks(2 * core + gg) for gg in range(2)]
+    own = [
+        [pick([one(lcoef.at[i], o) for o in range(4)], own_masks[gg]) for i in range(3)]
+        for gg in range(2)
+    ]
+    pair_rows.wait_recv()
+    for i in range(HALF):
+        low_k, high_k, _ = own[i // 6]
+        a_mine, b_mine = m1[core * HALF + i, 0:8, :], m1[core * HALF + i, 8:16, :]
+        a_other, b_other = other[i, 0:8, :], other[i, 8:16, :]
+        t = jnp.where(on_low, a_mine, a_other) + jnp.where(on_low, b_other, b_mine)
+        middle[i] = t
+        chip_rows[i, 0:8, :] = jnp.where(on_low, a_other, a_mine) + high_k * t
+        chip_rows[i, 8:16, :] = jnp.where(on_low, b_mine, b_other) + low_k * t
+
+    def solver_of(i, w, m):
+        b = (m + core) // 2
+        return w * 2 + b, m - b * (2 - core)
+
+    def targets():
+        for n, dw in enumerate((2, 1, 3, 0)):
+            w = lax.rem(z // 2 + dw, chips // 2)
+            for m in range(3):
+                zz, j = solver_of(None, w, m)
+                yield n * 3 + m, zz, j, w * 3 + m
+
+    def target_copy(n, zz, j, unit):
+        return remote(chip_rows.at[unit], r1.at[j, z], s1_sem.at[n], r1_sem.at[j, z], same_core(zz))
+
+    for n, zz, j, unit in targets():
+        @pl.when(zz != z)
+        def _():
+            target_copy(n, zz, j, unit).start()
+
+        @pl.when(zz == z)
+        def _():
+            r1[j, z] = chip_rows[unit]
 
     shift_high = pltpu.roll(wide_high, 1, 1)
     inner = jnp.logical_and(lane4 > 0, lane4 < levels - 1)
@@ -281,19 +336,19 @@
     for q in range(6):
         sol[levels - 1, q] = jnp.zeros((LINES, 128), f32)
 
-    crecv[me] = cmsg[...]
-    for step, flip in order:
-        peer = peer_at(step, flip)
-        remote(cmsg, crecv.at[peer], cs_sem.at[0], cr_sem.at[peer], to_depth(peer)).wait_recv()
+    crecv[z] = chip[...]
+    for step in steps:
+        zz = chip_at(step)
+        remote(chip, crecv.at[zz], cs_sem.at[0], cr_sem.at[zz], same_core(zz)).wait_recv()
     alphas, betas, crosses = [], [], []
-    for r in range(n_d):
+    for r in range(chips):
         tile = crecv[r]
-        alphas.append(jnp.broadcast_to(tile[:, 0:1], (8, 128)))
-        betas.append(jnp.broadcast_to(tile[:, 32:33], (8, 128)))
-        crosses.append(jnp.broadcast_to(tile[:, 64:65], (8, 128)))
-    mains = [1.0 + alphas[r] + (betas[r + 1] if r + 1 < n_d else 0.0) for r in range(n_d)]
+        alphas.append(splat(tile, 0))
+        betas.append(splat(tile, 32))
+        crosses.append(splat(tile, 64))
+    mains = [1.0 + alphas[r] + (betas[r + 1] if r + 1 < chips else 0.0) for r in range(chips)]
     before = None
-    for r in range(n_d):
+    for r in range(chips):
         q = crosses[r] * before if r > 0 else zero
         main = mains[r] - crosses[r] * q if r > 0 else mains[r]
         before = 1.0 / main
@@ -301,12 +356,21 @@
         comp[1, r] = before
         comp[4, r] = crosses[r]
     after = None
-    for r in range(n_d - 1, -1, -1):
-        q = crosses[r + 1] * after if r + 1 < n_d else zero
-        main = mains[r] - crosses[r + 1] * q if r + 1 < n_d else mains[r]
+    for r in range(chips - 1, -1, -1):
+        q = crosses[r + 1] * after if r + 1 < chips else zero
+        main = mains[r] - crosses[r + 1] * q if r + 1 < chips else mains[r]
         after = 1.0 / main
         comp[2, r] = q
         comp[3, r] = main
+
+    parity = lax.rem(z, 2)
+    first_unit = (z // 2) * 3 + parity * (2 - core)
+    has = [None, parity == core]
+    for j in range(2):
+        m = group_masks(2 * core + jnp.minimum(first_unit + j, HALF - 1) // 6)
+        for i in range(2):
+            for r in range(chips):
+                ucoef[j, i, r] = pick([one(comp.at[i, r], o) for o in range(4)], m)
 
     for copy in halo:
         copy.wait_recv()
@@ -314,16 +378,6 @@
     m_first = jnp.where(jnp.logical_and(third == 0, sub < 6), 0.25, 0.0).astype(f32)
     m_third = jnp.where(jnp.logical_and(third == 2, sub < 6), 0.25, 0.0).astype(f32)
     edge_line = (0, LINES - 1)
-    edge_off = [offv[0], offv[LINES - 1]]
-    me_low = jnp.maximum(me - 1, 0)
-
-    def one(ref, line):
-        return jnp.broadcast_to(ref[line:line + 1, :], (8, 128))
-
-    def edge_comp(i, r, e):
-        return jnp.broadcast_to(comp[i, r, pl.ds(edge_off[e], 1), :], (8, 128))
-
-    edge_sums = []
     for e in range(2):
         sign = 1.0 if e == 0 else -1.0
         line = edge_line[e]
@@ -339,62 +393,66 @@
             delta[e, k] = change
             sum_a[k % 2] = sum_a[k % 2] + one(high.at[k], line) * change
             sum_b[k % 2] = sum_b[k % 2] + one(low.at[k], line) * change
-        sum_a = sum_a[0] + sum_a[1]
-        sum_b = sum_b[0] + sum_b[1]
-        edge_sums.append((sum_a, sum_b))
-        em[0, 8 * e:8 * e + 8, :] = sum_a + edge_comp(0, me, e) * sum_b
-        em[1, 8 * e:8 * e + 8, :] = sum_b + edge_comp(2, me_low, e) * sum_a
-
-    def edge_copy(j, peer):
-        side = jnp.where(peer > me, 0, 1)
-        return remote(em.at[side], er.at[me], es_sem.at[j], er_sem.at[me], to_depth(peer))
-
-    for j, (step, flip) in enumerate(order):
-        edge_copy(j, peer_at(step, flip)).start()
-
-    quad, place = me // 4, lax.rem(me, 4)
-    has = [place != 3, place != 0]
-    units = [quad * 3 + jnp.minimum(place, 2), HALF + quad * 3 + jnp.maximum(place - 1, 0)]
-
-    for slot in range(2):
-        @pl.when(has[slot])
-        def _():
-            v = offl[units[slot] // 6]
-            m = [v == o for o in range(3)]
-            for i in range(2):
-                for r in range(n_d):
-                    ucoef[slot, i, r] = pick([one(comp.at[i, r], o) for o in range(4)], m)
-
-    def answer(slot, j, peer):
-        return remote(m2.at[slot, peer], back.at[units[slot]], s2_sem.at[slot, j],
-                      r2_sem.at[units[slot]], to_depth(peer))
-
-    for slot in range(2):
-        @pl.when(has[slot])
-        def _():
-            for step, flip in order:
-                peer = peer_at(step, flip)
-                remote(m1.at[0], r1.at[slot, peer], s1_sem.at[0], r1_sem.at[slot, peer],
-                       to_depth(peer)).wait_recv()
-            value = None
-            values = []
-            for r in range(n_d):
-                t = r1[slot, r, 0:8, :]
-                if r + 1 < n_d:
-                    t = t + r1[slot, r + 1, 8:16, :]
-                value = t if r == 0 else t + ucoef[slot, 0, r] * value
-                values.append(value)
-            s = values[n_d - 1] * ucoef[slot, 1, n_d - 1]
-            for r in range(n_d - 1, -1, -1):
-                m2[slot, r, 8:16, :] = s
-                if r + 1 < n_d:
-                    m2[slot, r + 1, 0:8, :] = s
-                if r > 0:
-                    s = values[r - 1] * ucoef[slot, 1, r - 1] + ucoef[slot, 0, r] * s
-            m2[slot, 0, 0:8, :] = zero
-            for j, (step, flip) in enumerate(order):
-                answer(slot, j, peer_at(step, flip)).start()
-            back[units[slot]] = m2[slot, me]
+        esum[e, 0:8, :] = sum_a[0] + sum_a[1]
+        esum[e, 8:16, :] = sum_b[0] + sum_b[1]
+    pair_edge = remote(esum.at[1 - core], epart, pair_send.at[2], pair_recv.at[2], partner)
+    pair_edge.start()
+
+    def answer(j, n, zz):
+        return remote(m2.at[j, zz], got.at[first_unit + j], s2_sem.at[j, n], r2_sem.at[first_unit + j],
+                      same_core(zz))
+
+    def solve_unit(j):
+        for step in steps:
+            zz = chip_at(step)
+            remote(chip_rows.at[0], r1.at[j, zz], s1_sem.at[0], r1_sem.at[j, zz], same_core(zz)).wait_recv()
+        values = []
+        for r in range(chips):
+            t = r1[j, r, 0:8, :]
+            if r + 1 < chips:
+                t = t + r1[j, r + 1, 8:16, :]
+            values.append(t if r == 0 else t + ucoef[j, 0, r] * values[r - 1])
+        s = values[chips - 1] * ucoef[j, 1, chips - 1]
+        for r in range(chips - 1, -1, -1):
+            m2[j, r, 8:16, :] = s
+            if r + 1 < chips:
+                m2[j, r + 1, 0:8, :] = s
+            if r > 0:
+                s = values[r - 1] * ucoef[j, 1, r - 1] + ucoef[j, 0, r] * s
+        m2[j, 0, 0:8, :] = zero
+        for n, step in enumerate(steps):
+            answer(j, n, chip_at(step)).start()
+        got[first_unit + j] = m2[j, z]
+
+    solve_unit(0)
+
+    @pl.when(has[1])
+    def _():
+        solve_unit(1)
+
+    edge_off = offv[core * (LINES - 1)]
+    z_low = jnp.maximum(z - 1, 0)
+
+    def edge_comp(i, r):
+        return jnp.broadcast_to(comp[i, r, pl.ds(edge_off, 1), :], (8, 128))
+
+    def edge_local(i):
+        return jnp.broadcast_to(lcoef[i, pl.ds(edge_off, 1), :], (8, 128))
+
+    pair_edge.wait_recv()
+    a_mine, b_mine = esum[core, 0:8, :], esum[core, 8:16, :]
+    a_other, b_other = epart[0:8, :], epart[8:16, :]
+    edge_t = jnp.where(on_low, a_mine, a_other) + jnp.where(on_low, b_other, b_mine)
+    edge_a = jnp.where(on_low, a_other, a_mine) + edge_local(1) * edge_t
+    edge_b = jnp.where(on_low, b_mine, b_other) + edge_local(0) * edge_t
+    em[0] = edge_a + edge_comp(0, z) * edge_b
+    em[1] = edge_b + edge_comp(2, z_low) * edge_a
+
+    def edge_copy(n, zz):
+        return remote(em.at[jnp.where(zz > z, 0, 1)], er.at[z], es_sem.at[n], er_sem.at[z], same_core(zz))
+
+    for n, step in enumerate(steps):
+        edge_copy(n, chip_at(step)).start()
 
     sol2 = sol.reshape(levels * 6 * LINES, 128)
     for e in range(2):
@@ -409,57 +467,66 @@
             rows = pl.ds(k * 6 * LINES + line, 6, stride=LINES)
             sol2[rows, :] = sol2[rows, :] + x[0:6, :]
 
-    for step, flip in order:
-        peer = peer_at(step, flip)
-        remote(em.at[0], er.at[peer], es_sem.at[0], er_sem.at[peer], to_depth(peer)).wait_recv()
-    edge_values = []
+    for step in steps:
+        zz = chip_at(step)
+        remote(em.at[0], er.at[zz], es_sem.at[0], er_sem.at[zz], same_core(zz)).wait_recv()
+    v = zero
+    w = zero
+    for r in range(chips):
+        v = jnp.where(r < z, er[r] + edge_comp(0, r) * v, v)
+    for r in range(chips - 1, 0, -1):
+        w = jnp.where(r > z, er[r] + edge_comp(2, r - 1) * w, w)
+    v = v + edge_b
+    w = w + edge_a
+    q_here = edge_comp(0, z)
+    u_here = edge_comp(4, z)
+    edge_high = (w + q_here * v) / (edge_comp(3, z) - u_here * q_here)
+    edge_low = jnp.where(z > 0, (v + u_here * edge_high) * edge_comp(1, z_low), 0.0)
+
+    for i in range(HALF):
+        @pl.when(w_solver(i, core) != z)
+        def _():
+            remote(m2.at[0, 0], got.at[i], s2_sem.at[0, 0], r2_sem.at[i], same_core(w_solver(i, core))).wait_recv()
+    got2 = got.reshape((HALF + 2) * 16, 128)
+    middle2 = middle.reshape((HALF + 2) * 8, 128)
     for e in range(2):
-        v = zero
-        w = zero
-        rows = slice(8 * e, 8 * e + 8)
-        for r in range(n_d):
-            v = jnp.where(r < me, er[r, rows, :] + edge_comp(0, r, e) * v, v)
-        for r in range(n_d - 1, 0, -1):
-            w = jnp.where(r > me, er[r, rows, :] + edge_comp(2, r - 1, e) * w, w)
-        v = v + edge_sums[e][1]
-        w = w + edge_sums[e][0]
-        q_me = edge_comp(0, me, e)
-        u_me = edge_comp(4, me, e)
-        s_here = (w + q_me * v) / (edge_comp(3, me, e) - u_me * q_me)
-        s_before = (v + u_me * s_here) * edge_comp(1, me_low, e)
-        edge_values.append((jnp.where(me > 0, s_before, 0.0), s_here))
-
-    for slot in range(2):
-        for unit in range(slot * HALF, (slot + 1) * HALF):
-            i = unit - slot * HALF
-            peer, _ = solver_of(slot, i // 3, i % 3)
-
-            @pl.when(me != peer)
-            def _():
-                remote(m2.at[slot, 0], back.at[unit], s2_sem.at[slot, 0], r2_sem.at[unit],
-                       to_depth(peer)).wait_recv()
-    back2 = back.reshape((UNITS + 2) * 16, 128)
-    for e in range(2):
-        unit0 = 0 if e == 0 else UNITS - 6
-        for w in range(2):
-            rows = pl.ds(unit0 * 16 + 8 * w + 7 * e, 6, stride=16)
-            back2[rows, :] = back2[rows, :] + edge_values[e][w][0:6, :]
-    for copy in halo:
+        @pl.when(core == e)
+        def _():
+            for ref, size, at, add in (
+                    (got2, 16, 0, edge_low), (got2, 16, 8, edge_high), (middle2, 8, 0, edge_t)):
+                rows = pl.ds(6 * e * size + at + 7 * e, 6, stride=size)
+                ref[rows, :] = ref[rows, :] + add[0:6, :]
+    for i in range(HALF):
+        low_k, high_k, pivot_k = own[i // 6]
+        s_low, s_high = got[i, 0:8, :], got[i, 8:16, :]
+        s_mid = middle[i] * pivot_k + low_k * s_low + high_k * s_high
+        back[core * HALF + i, 0:8, :] = jnp.where(on_low, s_low, s_mid)
+        back[core * HALF + i, 8:16, :] = jnp.where(on_low, s_mid, s_high)
+        pass_on[i, 0:8, :] = jnp.where(on_low, s_mid, s_low)
+        pass_on[i, 8:16, :] = jnp.where(on_low, s_high, s_mid)
+    pair_ends = remote(pass_on, back.at[pl.ds(core * HALF, HALF)], pair_send.at[3], pair_recv.at[3], partner)
+    pair_ends.start()
+
+    for copy in (*halo, pair_coef, pair_rows, pair_edge):
         copy.wait_send()
-    for j, (step, flip) in enumerate(order):
-        peer = peer_at(step, flip)
-        coef_copy(j, peer).wait_send()
-        edge_copy(j, peer).wait_send()
-    for slot in range(2):
-        for j, peer, unit in targets(slot):
-            @pl.when(peer != me)
-            def _():
-                target_copy(slot, j, peer, unit).wait_send()
-
-        @pl.when(has[slot])
+    for n, step in enumerate(steps):
+        coef_copy(n, chip_at(step)).wait_send()
+        edge_copy(n, chip_at(step)).wait_send()
+        answer(0, n, chip_at(step)).wait_send()
+    for n, zz, j, unit in targets():
+        @pl.when(zz != z)
         def _():
-            for j, (step, flip) in enumerate(order):
-                answer(slot, j, peer_at(step, flip)).wait_send()
+            target_copy(n, zz, j, unit).wait_send()
+
+    @pl.when(has[1])
+    def _():
+        for n, step in enumerate(steps):
+            answer(1, n, chip_at(step)).wait_send()
+    pair_ends.wait()
+
+
+def w_solver(i, core):
+    return (i // 3) * 2 + (i % 3 + core) // 2
 
 
 def assemble_kernel(sol, back, low, high, out, stage, sem):
@@ -498,6 +565,7 @@
 def body(n_h, n_d, fields, diffusivity, offsets, coupling, inverse):
     f32 = jnp.float32
     levels = fields.shape[1]
+    chips = n_d // 2
     hbm_spec = pl.BlockSpec(memory_space=pltpu.HBM)
     vmem_spec = pl.BlockSpec(memory_space=pltpu.VMEM)
     V = lambda *shape: pltpu.VMEM(shape, f32)
@@ -506,7 +574,7 @@
         functools.partial(columns_kernel, n_h, n_d),
         out_shape=(
             V(levels, 6, LINES, 128),
-            V(UNITS + 2, 16, 128),
+            V(UNITS, 16, 128),
             V(levels, LINES, 128),
             V(levels, LINES, 128),
         ),
@@ -525,27 +593,39 @@
             V(2, levels * 6, 128),
             V(2, levels * 6 + 16, 128),
             V(8, 128),
-            V(n_d, 8, 128),
+            V(8, 128),
+            V(8, 128),
+            V(chips, 8, 128),
             V(UNITS, 16, 128),
-            V(2, n_d, 16, 128),
-            V(2, n_d, 16, 128),
+            V(HALF, 16, 128),
+            V(HALF, 16, 128),
+            V(HALF + 2, 8, 128),
+            V(2, chips, 16, 128),
+            V(2, chips, 16, 128),
+            V(HALF + 2, 16, 128),
+            V(HALF, 16, 128),
             V(2, 16, 128),
-            V(n_d, 16, 128),
-            V(5, n_d, 8, 128),
-            V(2, 2, n_d, 8, 128),
+            V(16, 128),
+            V(2, 8, 128),
+            V(chips, 8, 128),
+            V(5, chips, 8, 128),
+            V(2, 2, chips, 8, 128),
+            V(3, 8, 128),
             dma(2, 6),
             dma(CHUNKS, 8),
             dma(3),
             dma(2),
             dma(2),
-            dma(n_d),
-            dma(n_d),
-            dma(UNITS),
-            dma(2, n_d),
-            dma(2, n_d),
-            dma(UNITS),
-            dma(n_d),
-            dma(n_d),
+            dma(4),
+            dma(4),
+            dma(chips),
+            dma(chips),
+            dma(HALF),
+            dma(2, chips),
+            dma(2, chips),
+            dma(HALF),
+            dma(chips),
+            dma(chips),
         ],
         compiler_params=pltpu.CompilerParams(
             collective_id=0, has_side_effects=True, vmem_limit_bytes=48 * 1024 * 1024),

time: 29.8 us -> 27 us (0.906)
  Pallas kernels: 29.7 us -> 27 us
    pallas_call x1, Pallas kernels: 27.7 us -> 25 us  [body(): pl.pallas_call(functools.partial(columns_kernel, n_h, n_d), out_shape=(V(...]
where the time goes in v3:
time: 27 us
  Pallas kernels  27 us (100%)
    pallas_call x1, Pallas kernels, body(): pl.pallas_call(functools.partial(columns_kernel, n_h, n_d), out_shape=(V(...  25 us
    pallas_call x1, Pallas kernels, body(): pl.pallas_call(assemble_kernel, out_shape=jax.ShapeDtypeStruct(fields.sha...  1.98 us

profile of v3, /device:TPU:1, one launch (start us, length us, event | category | flops | bytes accessed | tf_op | source)
XLA Modules:
  0.0 27.0 jit_solution(5498396345328404039)
XLA Ops:
  0.0 25.0 %columns.1 = (f32[32,6,32,128]{3,2,1,0:T(8,128)S(1)}, f32[24,16,128]{2,1,0:T(8,128)S(1)}, f32[32,32,128]{2,1,0:T(8,128)S(1)}, f32[32,32,128]{2,1,0:T(8,128)S(1)}) custom-call(f32[3,32,32,256]{3,2,1,0:T(8,128)} %fields.1, f32[32,32,256]{2,1,0:T(8,128)} %diff.1, s32[32]{0:T(128)} %offs.1, f32[4,32]{1,0:T(4,128)} %coup.1, f32[4,32,32]{2,1,0:T(8,128)} %inv.1), custom_call_target="tpu_custom_call" | custom-call | tf_op jit(solution)/shard_map/columns/pallas_call | solution.py:573
  25.0 2.0 %assemble.1 = f32[3,32,32,256]{3,2,1,0:T(8,128)} custom-call(f32[32,6,32,128]{3,2,1,0:T(8,128)S(1)} %get-tuple-element.9.sol, f32[24,16,128]{2,1,0:T(8,128)S(1)} %get-tuple-element.10.back, f32[32,32,128]{2,1,0:T(8,128)S(1)} %get-tuple-element.11.low, f32[32,32,128]{2,1,0:T(8,128)S(1)} %get-tuple-element.12.high), custom_call_target="tpu_custom_call" | custom-call | tf_op jit(solution)/shard_map/assemble/pallas_call | solution.py:635

commit v4 on v3

--- a/solution.py
+++ b/solution.py
@@ -28,7 +28,7 @@
     hsend, hrecv, cmsg, cpart, chip, crecv, m1, other, chip_rows, middle, r1, m2, got, pass_on,
     esum, epart, em, er, comp, ucoef, lcoef,
     edge_sem, load_sem, small_sem, hs_sem, hr_sem, pair_send, pair_recv, cs_sem, cr_sem,
-    s1_sem, r1_sem, s2_sem, r2_sem, es_sem, er_sem,
+    s1_sem, r1_sem, s2_sem, r2_sem, es_sem, er_sem, gate,
 ):
     f32 = jnp.float32
     levels = fields.shape[1]
@@ -55,7 +55,7 @@
             src_ref=src, dst_ref=dst, send_sem=send, recv_sem=recv, device_id=to, device_id_type=MESH)
 
     barrier = pltpu.get_barrier_semaphore()
-    meets = [(east, me), (west, me), partner] + [same_core(chip_at(step)) for step in steps]
+    meets = [(east, z * 2), (west, z * 2), partner] + [(me_h, chip_at(step) * 2 + 1) for step in steps]
     for to in meets:
         pl.semaphore_signal(barrier, inc=1, device_id=to, device_id_type=MESH)
 
@@ -121,8 +121,8 @@
     last_row = kvec[:, levels - 2, :]
     c_low = couple[:, 0:1]
     c_high = couple[:, levels - 1:levels]
-    gate = jnp.where(me > 0, 1.0, 0.0).astype(f32)
-    table_low = first_row * (jnp.broadcast_to(c_low, (4, levels)) * gate)
+    inside = jnp.where(me > 0, 1.0, 0.0).astype(f32)
+    table_low = first_row * (jnp.broadcast_to(c_low, (4, levels)) * inside)
     table_high = last_row * jnp.broadcast_to(c_high, (4, levels))
     lane4 = lax.broadcasted_iota(jnp.int32, (4, 128), 1)
 
@@ -218,8 +218,17 @@
     ]
     pair_coef = remote(cmsg, cpart, pair_send.at[0], pair_recv.at[0], partner)
     pair_rows = remote(m1.at[pl.ds((1 - core) * HALF, HALF)], other, pair_send.at[1], pair_recv.at[1], partner)
-    pl.semaphore_wait(barrier, len(meets))
-    for copy in (pair_coef, pair_rows, *halo):
+
+    @pl.when(core == 1)
+    def _():
+        pl.semaphore_wait(barrier, 2 * len(steps) + 1)
+        pl.semaphore_signal(gate.at[0], inc=1, device_id=partner, device_id_type=MESH)
+
+    @pl.when(core == 0)
+    def _():
+        pl.semaphore_wait(gate.at[0], 1)
+
+    for copy in (pair_coef, pair_rows):
         copy.start()
     for slot in range(2):
         @pl.when(core == slot)
@@ -295,6 +304,18 @@
         @pl.when(zz == z)
         def _():
             r1[j, z] = chip_rows[unit]
+
+    @pl.when(core == 0)
+    def _():
+        pl.semaphore_wait(barrier, 5)
+        pl.semaphore_signal(gate.at[1], inc=1, device_id=partner, device_id_type=MESH)
+
+    @pl.when(core == 1)
+    def _():
+        pl.semaphore_wait(gate.at[1], 1)
+
+    for copy in halo:
+        copy.start()
 
     shift_high = pltpu.roll(wide_high, 1, 1)
     inner = jnp.logical_and(lane4 > 0, lane4 < levels - 1)
@@ -626,6 +647,7 @@
             dma(HALF),
             dma(chips),
             dma(chips),
+            pltpu.SemaphoreType.REGULAR((2,)),
         ],
         compiler_params=pltpu.CompilerParams(
             collective_id=0, has_side_effects=True, vmem_limit_bytes=48 * 1024 * 1024),

time: 27 us -> 30.1 us (1.11)
  Pallas kernels: 27 us -> 30.1 us
    pallas_call x1, Pallas kernels: 25 us -> 28.1 us  [body(): pl.pallas_call(functools.partial(columns_kernel, n_h, n_d), out_shape=(V(...]
where the time goes in v4:
time: 30.1 us
  Pallas kernels  30.1 us (100%)
    pallas_call x1, Pallas kernels, body(): pl.pallas_call(functools.partial(columns_kernel, n_h, n_d), out_shape=(V(...  28.1 us
    pallas_call x1, Pallas kernels, body(): pl.pallas_call(assemble_kernel, out_shape=jax.ShapeDtypeStruct(fields.sha...  1.98 us

profile of v4, /device:TPU:1, one launch (start us, length us, event | category | flops | bytes accessed | tf_op | source)
XLA Modules:
  0.0 30.1 jit_solution(6653033855922946800)
XLA Ops:
  0.0 28.1 %columns.1 = (f32[32,6,32,128]{3,2,1,0:T(8,128)S(1)}, f32[24,16,128]{2,1,0:T(8,128)S(1)}, f32[32,32,128]{2,1,0:T(8,128)S(1)}, f32[32,32,128]{2,1,0:T(8,128)S(1)}) custom-call(f32[3,32,32,256]{3,2,1,0:T(8,128)} %fields.1, f32[32,32,256]{2,1,0:T(8,128)} %diff.1, s32[32]{0:T(128)} %offs.1, f32[4,32]{1,0:T(4,128)} %coup.1, f32[4,32,32]{2,1,0:T(8,128)} %inv.1), custom_call_target="tpu_custom_call" | custom-call | tf_op jit(solution)/shard_map/columns/pallas_call | solution.py:594
  28.1 2.0 %assemble.1 = f32[3,32,32,256]{3,2,1,0:T(8,128)} custom-call(f32[32,6,32,128]{3,2,1,0:T(8,128)S(1)} %get-tuple-element.9.sol, f32[24,16,128]{2,1,0:T(8,128)S(1)} %get-tuple-element.10.back, f32[32,32,128]{2,1,0:T(8,128)S(1)} %get-tuple-element.11.low, f32[32,32,128]{2,1,0:T(8,128)S(1)} %get-tuple-element.12.high), custom_call_target="tpu_custom_call" | custom-call | tf_op jit(solution)/shard_map/assemble/pallas_call | solution.py:657

commit v5 on v4

--- a/solution.py
+++ b/solution.py
@@ -156,6 +156,30 @@
         copy.wait()
     hsend[0] = f2[pl.ds(39, levels * 6, stride=PAD), :]
     hsend[1] = f2[pl.ds(8, levels * 6, stride=PAD), :]
+    halo = [
+        remote(hsend.at[e], hrecv.at[e, pl.ds(8, levels * 6), :], hs_sem.at[e], hr_sem.at[e], (to, me))
+        for e, to in ((0, east), (1, west))
+    ]
+
+    waits_late = lax.rem(me_h, 4) == 0
+
+    def send_halo():
+        @pl.when(core == 0)
+        def _():
+            pl.semaphore_wait(barrier, 5)
+            pl.semaphore_signal(gate.at[1], inc=1, device_id=partner, device_id_type=MESH)
+
+        @pl.when(core == 1)
+        def _():
+            pl.semaphore_wait(gate.at[1], 1)
+
+        for copy in halo:
+            copy.start()
+
+    @pl.when(jnp.logical_not(waits_late))
+    def _():
+        send_halo()
+
     is_last = lane == 127
     is_first = lane == 0
 
@@ -212,10 +236,6 @@
         def _():
             slot_forcing(slot, True)
 
-    halo = [
-        remote(hsend.at[e], hrecv.at[e, pl.ds(8, levels * 6), :], hs_sem.at[e], hr_sem.at[e], (to, me))
-        for e, to in ((0, east), (1, west))
-    ]
     pair_coef = remote(cmsg, cpart, pair_send.at[0], pair_recv.at[0], partner)
     pair_rows = remote(m1.at[pl.ds((1 - core) * HALF, HALF)], other, pair_send.at[1], pair_recv.at[1], partner)
 
@@ -305,17 +325,9 @@
         def _():
             r1[j, z] = chip_rows[unit]
 
-    @pl.when(core == 0)
+    @pl.when(waits_late)
     def _():
-        pl.semaphore_wait(barrier, 5)
-        pl.semaphore_signal(gate.at[1], inc=1, device_id=partner, device_id_type=MESH)
-
-    @pl.when(core == 1)
-    def _():
-        pl.semaphore_wait(gate.at[1], 1)
-
-    for copy in halo:
-        copy.start()
+        send_halo()
 
     shift_high = pltpu.roll(wide_high, 1, 1)
     inner = jnp.logical_and(lane4 > 0, lane4 < levels - 1)
@@ -393,31 +405,37 @@
             for r in range(chips):
                 ucoef[j, i, r] = pick([one(comp.at[i, r], o) for o in range(4)], m)
 
-    for copy in halo:
-        copy.wait_recv()
     third = lax.rem(sub, 3)
     m_first = jnp.where(jnp.logical_and(third == 0, sub < 6), 0.25, 0.0).astype(f32)
     m_third = jnp.where(jnp.logical_and(third == 2, sub < 6), 0.25, 0.0).astype(f32)
     edge_line = (0, LINES - 1)
-    for e in range(2):
-        sign = 1.0 if e == 0 else -1.0
-        line = edge_line[e]
-        sum_a = [zero, zero]
-        sum_b = [zero, zero]
-        for k in range(levels):
-            r = 8 + 6 * k
-            here = hrecv[e, r:r + 8, :]
-            above = hrecv[e, r + 2:r + 10, :]
-            below = hrecv[e, r - 2:r + 6, :]
-            d = jnp.where(sub < 3, one(dbuf.at[k, 0], line), one(dbuf.at[k, 1], line))
-            change = d * here + sign * (m_first * above + m_third * below)
-            delta[e, k] = change
-            sum_a[k % 2] = sum_a[k % 2] + one(high.at[k], line) * change
-            sum_b[k % 2] = sum_b[k % 2] + one(low.at[k], line) * change
-        esum[e, 0:8, :] = sum_a[0] + sum_a[1]
-        esum[e, 8:16, :] = sum_b[0] + sum_b[1]
     pair_edge = remote(esum.at[1 - core], epart, pair_send.at[2], pair_recv.at[2], partner)
-    pair_edge.start()
+
+    def halo_sums():
+        for copy in halo:
+            copy.wait_recv()
+        for e in range(2):
+            sign = 1.0 if e == 0 else -1.0
+            line = edge_line[e]
+            sum_a = [zero, zero]
+            sum_b = [zero, zero]
+            for k in range(levels):
+                r = 8 + 6 * k
+                here = hrecv[e, r:r + 8, :]
+                above = hrecv[e, r + 2:r + 10, :]
+                below = hrecv[e, r - 2:r + 6, :]
+                d = jnp.where(sub < 3, one(dbuf.at[k, 0], line), one(dbuf.at[k, 1], line))
+                change = d * here + sign * (m_first * above + m_third * below)
+                delta[e, k] = change
+                sum_a[k % 2] = sum_a[k % 2] + one(high.at[k], line) * change
+                sum_b[k % 2] = sum_b[k % 2] + one(low.at[k], line) * change
+            esum[e, 0:8, :] = sum_a[0] + sum_a[1]
+            esum[e, 8:16, :] = sum_b[0] + sum_b[1]
+        pair_edge.start()
+
+    @pl.when(me_h != 0)
+    def _():
+        halo_sums()
 
     def answer(j, n, zz):
         return remote(m2.at[j, zz], got.at[first_unit + j], s2_sem.at[j, n], r2_sem.at[first_unit + j],
@@ -450,6 +468,10 @@
     @pl.when(has[1])
     def _():
         solve_unit(1)
+
+    @pl.when(me_h == 0)
+    def _():
+        halo_sums()
 
     edge_off = offv[core * (LINES - 1)]
     z_low = jnp.maximum(z - 1, 0)

time: 30.1 us -> 26.1 us (0.87)
  Pallas kernels: 30.1 us -> 26 us
    pallas_call x1, Pallas kernels: 28.1 us -> 24 us  [body(): pl.pallas_call(functools.partial(columns_kernel, n_h, n_d), out_shape=(V(...]
where the time goes in v5:
time: 26.1 us; the launch traced here: 26 us
  Pallas kernels  26 us (100%)
    pallas_call x1, Pallas kernels, body(): pl.pallas_call(functools.partial(columns_kernel, n_h, n_d), out_shape=(V(...  24 us
    pallas_call x1, Pallas kernels, body(): pl.pallas_call(assemble_kernel, out_shape=jax.ShapeDtypeStruct(fields.sha...  1.98 us

profile of v5, /device:TPU:1, one launch (start us, length us, event | category | flops | bytes accessed | tf_op | source)
XLA Modules:
  0.0 26.0 jit_solution(9104169656195454970)
XLA Ops:
  0.0 24.0 %columns.1 = (f32[32,6,32,128]{3,2,1,0:T(8,128)S(1)}, f32[24,16,128]{2,1,0:T(8,128)S(1)}, f32[32,32,128]{2,1,0:T(8,128)S(1)}, f32[32,32,128]{2,1,0:T(8,128)S(1)}) custom-call(f32[3,32,32,256]{3,2,1,0:T(8,128)} %fields.1, f32[32,32,256]{2,1,0:T(8,128)} %diff.1, s32[32]{0:T(128)} %offs.1, f32[4,32]{1,0:T(4,128)} %coup.1, f32[4,32,32]{2,1,0:T(8,128)} %inv.1), custom_call_target="tpu_custom_call" | custom-call | tf_op jit(solution)/shard_map/columns/pallas_call | solution.py:616
  24.0 2.0 %assemble.1 = f32[3,32,32,256]{3,2,1,0:T(8,128)} custom-call(f32[32,6,32,128]{3,2,1,0:T(8,128)S(1)} %get-tuple-element.9.sol, f32[24,16,128]{2,1,0:T(8,128)S(1)} %get-tuple-element.10.back, f32[32,32,128]{2,1,0:T(8,128)S(1)} %get-tuple-element.11.low, f32[32,32,128]{2,1,0:T(8,128)S(1)} %get-tuple-element.12.high), custom_call_target="tpu_custom_call" | custom-call | tf_op jit(solution)/shard_map/assemble/pallas_call | solution.py:679

commit v6 on v4

--- a/solution.py
+++ b/solution.py
@@ -26,7 +26,7 @@
     sol, back, low, high,
     fbuf, dbuf, offv, cvec, kvec, offl, wv, iv, delta,
     hsend, hrecv, cmsg, cpart, chip, crecv, m1, other, chip_rows, middle, r1, m2, got, pass_on,
-    esum, epart, em, er, comp, ucoef, lcoef,
+    esum, epart, em, er, comp, ucoef, lcoef, ends,
     edge_sem, load_sem, small_sem, hs_sem, hr_sem, pair_send, pair_recv, cs_sem, cr_sem,
     s1_sem, r1_sem, s2_sem, r2_sem, es_sem, er_sem, gate,
 ):
@@ -101,6 +101,37 @@
         hrecv[e, 200:208, :] = jnp.zeros((8, 128), f32)
     m1[...] = jnp.zeros(m1.shape, f32)
 
+    def pack():
+        for copy in outer:
+            copy.wait()
+        hsend[0] = f2[pl.ds(39, levels * 6, stride=PAD), :]
+        hsend[1] = f2[pl.ds(8, levels * 6, stride=PAD), :]
+
+    halo = [
+        remote(hsend.at[e], hrecv.at[e, pl.ds(8, levels * 6), :], hs_sem.at[e], hr_sem.at[e], (to, me))
+        for e, to in ((0, east), (1, west))
+    ]
+
+    waits_late = me_h == 0
+
+    def send_halo():
+        @pl.when(core == 0)
+        def _():
+            pl.semaphore_wait(barrier, 5)
+            pl.semaphore_signal(gate.at[1], inc=1, device_id=partner, device_id_type=MESH)
+
+        @pl.when(core == 1)
+        def _():
+            pl.semaphore_wait(gate.at[1], 1)
+
+        for copy in halo:
+            copy.start()
+
+    @pl.when(me_h == n_h - 1)
+    def _():
+        pack()
+        send_halo()
+
     for copy in small:
         copy.wait()
     sub = lax.broadcasted_iota(jnp.int32, (8, 128), 0)
@@ -152,10 +183,14 @@
     cmsg[0:4, :] = packed
     cmsg[4:8, :] = packed
 
-    for copy in outer:
-        copy.wait()
-    hsend[0] = f2[pl.ds(39, levels * 6, stride=PAD), :]
-    hsend[1] = f2[pl.ds(8, levels * 6, stride=PAD), :]
+    @pl.when(me_h != n_h - 1)
+    def _():
+        pack()
+
+    @pl.when(jnp.logical_and(me_h != n_h - 1, jnp.logical_not(waits_late)))
+    def _():
+        send_halo()
+
     is_last = lane == 127
     is_first = lane == 0
 
@@ -212,10 +247,6 @@
         def _():
             slot_forcing(slot, True)
 
-    halo = [
-        remote(hsend.at[e], hrecv.at[e, pl.ds(8, levels * 6), :], hs_sem.at[e], hr_sem.at[e], (to, me))
-        for e, to in ((0, east), (1, west))
-    ]
     pair_coef = remote(cmsg, cpart, pair_send.at[0], pair_recv.at[0], partner)
     pair_rows = remote(m1.at[pl.ds((1 - core) * HALF, HALF)], other, pair_send.at[1], pair_recv.at[1], partner)
 
@@ -305,17 +336,9 @@
         def _():
             r1[j, z] = chip_rows[unit]
 
-    @pl.when(core == 0)
-    def _():
-        pl.semaphore_wait(barrier, 5)
-        pl.semaphore_signal(gate.at[1], inc=1, device_id=partner, device_id_type=MESH)
-
-    @pl.when(core == 1)
-    def _():
-        pl.semaphore_wait(gate.at[1], 1)
-
-    for copy in halo:
-        copy.start()
+    @pl.when(waits_late)
+    def _():
+        send_halo()
 
     shift_high = pltpu.roll(wide_high, 1, 1)
     inner = jnp.logical_and(lane4 > 0, lane4 < levels - 1)
@@ -356,6 +379,38 @@
     lax.fori_loop(0, levels - 1, rise, (zero,) * UNITS)
     for q in range(6):
         sol[levels - 1, q] = jnp.zeros((LINES, 128), f32)
+
+    third = lax.rem(sub, 3)
+    m_first = jnp.where(jnp.logical_and(third == 0, sub < 6), 0.25, 0.0).astype(f32)
+    m_third = jnp.where(jnp.logical_and(third == 2, sub < 6), 0.25, 0.0).astype(f32)
+    edge_line = (0, LINES - 1)
+    pair_edge = remote(esum.at[1 - core], epart, pair_send.at[2], pair_recv.at[2], partner)
+
+    def halo_sums():
+        for copy in halo:
+            copy.wait_recv()
+        for e in range(2):
+            sign = 1.0 if e == 0 else -1.0
+            line = edge_line[e]
+            sum_a = [zero, zero]
+            sum_b = [zero, zero]
+            for k in range(levels):
+                r = 8 + 6 * k
+                here = hrecv[e, r:r + 8, :]
+                above = hrecv[e, r + 2:r + 10, :]
+                below = hrecv[e, r - 2:r + 6, :]
+                d = jnp.where(sub < 3, one(dbuf.at[k, 0], line), one(dbuf.at[k, 1], line))
+                change = d * here + sign * (m_first * above + m_third * below)
+                delta[e, k] = change
+                sum_a[k % 2] = sum_a[k % 2] + one(high.at[k], line) * change
+                sum_b[k % 2] = sum_b[k % 2] + one(low.at[k], line) * change
+            esum[e, 0:8, :] = sum_a[0] + sum_a[1]
+            esum[e, 8:16, :] = sum_b[0] + sum_b[1]
+        pair_edge.start()
+
+    @pl.when(me_h > 1)
+    def _():
+        halo_sums()
 
     crecv[z] = chip[...]
     for step in steps:
@@ -393,31 +448,36 @@
             for r in range(chips):
                 ucoef[j, i, r] = pick([one(comp.at[i, r], o) for o in range(4)], m)
 
-    for copy in halo:
-        copy.wait_recv()
-    third = lax.rem(sub, 3)
-    m_first = jnp.where(jnp.logical_and(third == 0, sub < 6), 0.25, 0.0).astype(f32)
-    m_third = jnp.where(jnp.logical_and(third == 2, sub < 6), 0.25, 0.0).astype(f32)
-    edge_line = (0, LINES - 1)
-    for e in range(2):
-        sign = 1.0 if e == 0 else -1.0
-        line = edge_line[e]
-        sum_a = [zero, zero]
-        sum_b = [zero, zero]
-        for k in range(levels):
-            r = 8 + 6 * k
-            here = hrecv[e, r:r + 8, :]
-            above = hrecv[e, r + 2:r + 10, :]
-            below = hrecv[e, r - 2:r + 6, :]
-            d = jnp.where(sub < 3, one(dbuf.at[k, 0], line), one(dbuf.at[k, 1], line))
-            change = d * here + sign * (m_first * above + m_third * below)
-            delta[e, k] = change
-            sum_a[k % 2] = sum_a[k % 2] + one(high.at[k], line) * change
-            sum_b[k % 2] = sum_b[k % 2] + one(low.at[k], line) * change
-        esum[e, 0:8, :] = sum_a[0] + sum_a[1]
-        esum[e, 8:16, :] = sum_b[0] + sum_b[1]
-    pair_edge = remote(esum.at[1 - core], epart, pair_send.at[2], pair_recv.at[2], partner)
-    pair_edge.start()
+    edge_off = offv[core * (LINES - 1)]
+    z_low = jnp.maximum(z - 1, 0)
+
+    def edge_comp(i, r):
+        return jnp.broadcast_to(comp[i, r, pl.ds(edge_off, 1), :], (8, 128))
+
+    def edge_local(i):
+        return jnp.broadcast_to(lcoef[i, pl.ds(edge_off, 1), :], (8, 128))
+
+    def edge_copy(n, zz):
+        return remote(em.at[jnp.where(zz > z, 0, 1)], er.at[z], es_sem.at[n], er_sem.at[z], same_core(zz))
+
+    def edge_send():
+        pair_edge.wait_recv()
+        a_mine, b_mine = esum[core, 0:8, :], esum[core, 8:16, :]
+        a_other, b_other = epart[0:8, :], epart[8:16, :]
+        edge_t = jnp.where(on_low, a_mine, a_other) + jnp.where(on_low, b_other, b_mine)
+        edge_a = jnp.where(on_low, a_other, a_mine) + edge_local(1) * edge_t
+        edge_b = jnp.where(on_low, b_mine, b_other) + edge_local(0) * edge_t
+        ends[0] = edge_t
+        ends[1] = edge_a
+        ends[2] = edge_b
+        em[0] = edge_a + edge_comp(0, z) * edge_b
+        em[1] = edge_b + edge_comp(2, z_low) * edge_a
+        for n, step in enumerate(steps):
+            edge_copy(n, chip_at(step)).start()
+
+    @pl.when(me_h > 1)
+    def _():
+        edge_send()
 
     def answer(j, n, zz):
         return remote(m2.at[j, zz], got.at[first_unit + j], s2_sem.at[j, n], r2_sem.at[first_unit + j],
@@ -451,29 +511,10 @@
     def _():
         solve_unit(1)
 
-    edge_off = offv[core * (LINES - 1)]
-    z_low = jnp.maximum(z - 1, 0)
-
-    def edge_comp(i, r):
-        return jnp.broadcast_to(comp[i, r, pl.ds(edge_off, 1), :], (8, 128))
-
-    def edge_local(i):
-        return jnp.broadcast_to(lcoef[i, pl.ds(edge_off, 1), :], (8, 128))
-
-    pair_edge.wait_recv()
-    a_mine, b_mine = esum[core, 0:8, :], esum[core, 8:16, :]
-    a_other, b_other = epart[0:8, :], epart[8:16, :]
-    edge_t = jnp.where(on_low, a_mine, a_other) + jnp.where(on_low, b_other, b_mine)
-    edge_a = jnp.where(on_low, a_other, a_mine) + edge_local(1) * edge_t
-    edge_b = jnp.where(on_low, b_mine, b_other) + edge_local(0) * edge_t
-    em[0] = edge_a + edge_comp(0, z) * edge_b
-    em[1] = edge_b + edge_comp(2, z_low) * edge_a
-
-    def edge_copy(n, zz):
-        return remote(em.at[jnp.where(zz > z, 0, 1)], er.at[z], es_sem.at[n], er_sem.at[z], same_core(zz))
-
-    for n, step in enumerate(steps):
-        edge_copy(n, chip_at(step)).start()
+    @pl.when(me_h <= 1)
+    def _():
+        halo_sums()
+        edge_send()
 
     sol2 = sol.reshape(levels * 6 * LINES, 128)
     for e in range(2):
@@ -497,8 +538,9 @@
         v = jnp.where(r < z, er[r] + edge_comp(0, r) * v, v)
     for r in range(chips - 1, 0, -1):
         w = jnp.where(r > z, er[r] + edge_comp(2, r - 1) * w, w)
-    v = v + edge_b
-    w = w + edge_a
+    edge_t = ends[0]
+    v = v + ends[2]
+    w = w + ends[1]
     q_here = edge_comp(0, z)
     u_here = edge_comp(4, z)
     edge_high = (w + q_here * v) / (edge_comp(3, z) - u_here * q_here)
@@ -558,8 +600,8 @@
         lev = pl.ds(c * per, per)
         return [
             pltpu.make_async_copy(
-                stage.at[lev, h * 3 + f], out.at[f, lev, :, pl.ds(h * 128, 128)], sem.at[c, h * 3 + f])
-            for h in range(2) for f in range(3)
+                stage.at[f, lev], out.at[f, lev], sem.at[c, f])
+            for f in range(3)
         ]
 
     def chunk(c, carry):
@@ -572,7 +614,8 @@
                 lo = low[k, rows, :]
                 hi = high[k, rows, :]
                 for q in range(6):
-                    stage[k, q, rows, :] = sol[k, q, rows, :] + (lo * prev[q] + hi * here[q])
+                    h, f = q // 3, q % 3
+                    stage[f, k, rows, 128 * h:128 * h + 128] = sol[k, q, rows, :] + (lo * prev[q] + hi * here[q])
         for copy in copies(c):
             copy.start()
         return carry
@@ -632,6 +675,7 @@
             V(5, chips, 8, 128),
             V(2, 2, chips, 8, 128),
             V(3, 8, 128),
+            V(3, 8, 128),
             dma(2, 6),
             dma(CHUNKS, 8),
             dma(3),
@@ -660,8 +704,8 @@
         in_specs=[vmem_spec] * 4,
         out_specs=hbm_spec,
         scratch_shapes=[
-            V(levels, 6, LINES, 128),
-            dma(CHUNKS, 6),
+            V(3, levels, LINES, 256),
+            dma(CHUNKS, 3),
         ],
         compiler_params=pltpu.CompilerParams(vmem_limit_bytes=48 * 1024 * 1024),
         name="assemble",

time: 30.1 us -> 25.7 us (0.85)
  Pallas kernels: 30.1 us -> 25.6 us
    pallas_call x1, Pallas kernels: 28.1 us -> 23.8 us  [body(): pl.pallas_call(functools.partial(columns_kernel, n_h, n_d), out_shape=(V(...]
where the time goes in v6:
time: 25.7 us; the launch traced here: 25.6 us
  Pallas kernels  25.6 us (100%)
    pallas_call x1, Pallas kernels, body(): pl.pallas_call(functools.partial(columns_kernel, n_h, n_d), out_shape=(V(...  23.8 us
    pallas_call x1, Pallas kernels, body(): pl.pallas_call(assemble_kernel, out_shape=jax.ShapeDtypeStruct(fields.sha...  1.87 us

profile of v6, /device:TPU:1, one launch (start us, length us, event | category | flops | bytes accessed | tf_op | source)
XLA Modules:
  0.0 25.6 jit_solution(13325305846982862644)
XLA Ops:
  0.0 23.8 %columns.1 = (f32[32,6,32,128]{3,2,1,0:T(8,128)S(1)}, f32[24,16,128]{2,1,0:T(8,128)S(1)}, f32[32,32,128]{2,1,0:T(8,128)S(1)}, f32[32,32,128]{2,1,0:T(8,128)S(1)}) custom-call(f32[3,32,32,256]{3,2,1,0:T(8,128)} %fields.1, f32[32,32,256]{2,1,0:T(8,128)} %diff.1, s32[32]{0:T(128)} %offs.1, f32[4,32]{1,0:T(4,128)} %coup.1, f32[4,32,32]{2,1,0:T(8,128)} %inv.1), custom_call_target="tpu_custom_call" | custom-call | tf_op jit(solution)/shard_map/columns/pallas_call | solution.py:637
  23.8 1.9 %assemble.1 = f32[3,32,32,256]{3,2,1,0:T(8,128)} custom-call(f32[32,6,32,128]{3,2,1,0:T(8,128)S(1)} %get-tuple-element.9.sol, f32[24,16,128]{2,1,0:T(8,128)S(1)} %get-tuple-element.10.back, f32[32,32,128]{2,1,0:T(8,128)S(1)} %get-tuple-element.11.low, f32[32,32,128]{2,1,0:T(8,128)S(1)} %get-tuple-element.12.high), custom_call_target="tpu_custom_call" | custom-call | tf_op jit(solution)/shard_map/assemble/pallas_call | solution.py:701

commit v7 on v6

--- a/solution.py
+++ b/solution.py
@@ -26,7 +26,7 @@
     sol, back, low, high,
     fbuf, dbuf, offv, cvec, kvec, offl, wv, iv, delta,
     hsend, hrecv, cmsg, cpart, chip, crecv, m1, other, chip_rows, middle, r1, m2, got, pass_on,
-    esum, epart, em, er, comp, ucoef, lcoef, ends,
+    esum, epart, em, er, comp, ucoef, lcoef, ends, edge_out, edge_in,
     edge_sem, load_sem, small_sem, hs_sem, hr_sem, pair_send, pair_recv, cs_sem, cr_sem,
     s1_sem, r1_sem, s2_sem, r2_sem, es_sem, er_sem, gate,
 ):
@@ -65,7 +65,7 @@
         pltpu.make_async_copy(inv, kvec, small_sem.at[2]),
     ]
     outer = []
-    for i, first in enumerate((0, LINES - 8)):
+    for i, first in enumerate((LINES - 8, 0)):
         for h in range(2):
             for f in range(3):
                 outer.append(pltpu.make_async_copy(
@@ -101,11 +101,10 @@
         hrecv[e, 200:208, :] = jnp.zeros((8, 128), f32)
     m1[...] = jnp.zeros(m1.shape, f32)
 
-    def pack():
-        for copy in outer:
+    def pack(e):
+        for copy in outer[6 * e:6 * e + 6]:
             copy.wait()
-        hsend[0] = f2[pl.ds(39, levels * 6, stride=PAD), :]
-        hsend[1] = f2[pl.ds(8, levels * 6, stride=PAD), :]
+        hsend[e] = f2[pl.ds(8 if e else 39, levels * 6, stride=PAD), :]
 
     halo = [
         remote(hsend.at[e], hrecv.at[e, pl.ds(8, levels * 6), :], hs_sem.at[e], hr_sem.at[e], (to, me))
@@ -114,7 +113,7 @@
 
     waits_late = me_h == 0
 
-    def send_halo():
+    def meet_neighbours():
         @pl.when(core == 0)
         def _():
             pl.semaphore_wait(barrier, 5)
@@ -124,13 +123,12 @@
         def _():
             pl.semaphore_wait(gate.at[1], 1)
 
-        for copy in halo:
-            copy.start()
-
     @pl.when(me_h == n_h - 1)
     def _():
-        pack()
-        send_halo()
+        meet_neighbours()
+        for e in range(2):
+            pack(e)
+            halo[e].start()
 
     for copy in small:
         copy.wait()
@@ -185,7 +183,13 @@
 
     @pl.when(me_h != n_h - 1)
     def _():
-        pack()
+        for e in range(2):
+            pack(e)
+
+    def send_halo():
+        meet_neighbours()
+        for copy in halo:
+            copy.start()
 
     @pl.when(jnp.logical_and(me_h != n_h - 1, jnp.logical_not(waits_late)))
     def _():
@@ -387,9 +391,8 @@
     pair_edge = remote(esum.at[1 - core], epart, pair_send.at[2], pair_recv.at[2], partner)
 
     def halo_sums():
-        for copy in halo:
-            copy.wait_recv()
-        for e in range(2):
+        for e in (1, 0):
+            halo[e].wait_recv()
             sign = 1.0 if e == 0 else -1.0
             line = edge_line[e]
             sum_a = [zero, zero]
@@ -529,6 +532,21 @@
             rows = pl.ds(k * 6 * LINES + line, 6, stride=LINES)
             sol2[rows, :] = sol2[rows, :] + x[0:6, :]
 
+    for i in range(HALF):
+        @pl.when(w_solver(i, core) != z)
+        def _():
+            remote(m2.at[0, 0], got.at[i], s2_sem.at[0, 0], r2_sem.at[i], same_core(w_solver(i, core))).wait_recv()
+    for i in range(HALF):
+        low_k, high_k, pivot_k = own[i // 6]
+        s_low, s_high = got[i, 0:8, :], got[i, 8:16, :]
+        s_mid = middle[i] * pivot_k + low_k * s_low + high_k * s_high
+        back[core * HALF + i, 0:8, :] = jnp.where(on_low, s_low, s_mid)
+        back[core * HALF + i, 8:16, :] = jnp.where(on_low, s_mid, s_high)
+        pass_on[i, 0:8, :] = jnp.where(on_low, s_mid, s_low)
+        pass_on[i, 8:16, :] = jnp.where(on_low, s_high, s_mid)
+    pair_ends = remote(pass_on, back.at[pl.ds(core * HALF, HALF)], pair_send.at[3], pair_recv.at[3], partner)
+    pair_ends.start()
+
     for step in steps:
         zz = chip_at(step)
         remote(em.at[0], er.at[zz], es_sem.at[0], er_sem.at[zz], same_core(zz)).wait_recv()
@@ -545,30 +563,22 @@
     u_here = edge_comp(4, z)
     edge_high = (w + q_here * v) / (edge_comp(3, z) - u_here * q_here)
     edge_low = jnp.where(z > 0, (v + u_here * edge_high) * edge_comp(1, z_low), 0.0)
-
-    for i in range(HALF):
-        @pl.when(w_solver(i, core) != z)
-        def _():
-            remote(m2.at[0, 0], got.at[i], s2_sem.at[0, 0], r2_sem.at[i], same_core(w_solver(i, core))).wait_recv()
-    got2 = got.reshape((HALF + 2) * 16, 128)
-    middle2 = middle.reshape((HALF + 2) * 8, 128)
+    edge_mid = edge_local(2) * edge_t + edge_local(0) * edge_low + edge_local(1) * edge_high
+    edge_out[0:8, :] = jnp.where(on_low, edge_mid, edge_low)
+    edge_out[8:16, :] = jnp.where(on_low, edge_high, edge_mid)
+    pair_last = remote(edge_out, edge_in, pair_send.at[4], pair_recv.at[4], partner)
+    pair_last.start()
+    back2 = back.reshape((UNITS + 2) * 16, 128)
+
+    def add_to_line(e, parts):
+        for w in range(2):
+            rows = pl.ds(e * (UNITS - 6) * 16 + 8 * w + 7 * e, 6, stride=16)
+            back2[rows, :] = back2[rows, :] + parts[w][0:6, :]
+
     for e in range(2):
         @pl.when(core == e)
         def _():
-            for ref, size, at, add in (
-                    (got2, 16, 0, edge_low), (got2, 16, 8, edge_high), (middle2, 8, 0, edge_t)):
-                rows = pl.ds(6 * e * size + at + 7 * e, 6, stride=size)
-                ref[rows, :] = ref[rows, :] + add[0:6, :]
-    for i in range(HALF):
-        low_k, high_k, pivot_k = own[i // 6]
-        s_low, s_high = got[i, 0:8, :], got[i, 8:16, :]
-        s_mid = middle[i] * pivot_k + low_k * s_low + high_k * s_high
-        back[core * HALF + i, 0:8, :] = jnp.where(on_low, s_low, s_mid)
-        back[core * HALF + i, 8:16, :] = jnp.where(on_low, s_mid, s_high)
-        pass_on[i, 0:8, :] = jnp.where(on_low, s_mid, s_low)
-        pass_on[i, 8:16, :] = jnp.where(on_low, s_high, s_mid)
-    pair_ends = remote(pass_on, back.at[pl.ds(core * HALF, HALF)], pair_send.at[3], pair_recv.at[3], partner)
-    pair_ends.start()
+            add_to_line(e, (edge_low, edge_mid) if e == 0 else (edge_mid, edge_high))
 
     for copy in (*halo, pair_coef, pair_rows, pair_edge):
         copy.wait_send()
@@ -586,6 +596,11 @@
         for n, step in enumerate(steps):
             answer(1, n, chip_at(step)).wait_send()
     pair_ends.wait()
+    pair_last.wait()
+    for e in range(2):
+        @pl.when(core == 1 - e)
+        def _():
+            add_to_line(e, (edge_in[0:8, :], edge_in[8:16, :]))
 
 
 def w_solver(i, core):
@@ -638,7 +653,7 @@
         functools.partial(columns_kernel, n_h, n_d),
         out_shape=(
             V(levels, 6, LINES, 128),
-            V(UNITS, 16, 128),
+            V(UNITS + 2, 16, 128),
             V(levels, LINES, 128),
             V(levels, LINES, 128),
         ),
@@ -676,13 +691,15 @@
             V(2, 2, chips, 8, 128),
             V(3, 8, 128),
             V(3, 8, 128),
+            V(16, 128),
+            V(16, 128),
             dma(2, 6),
             dma(CHUNKS, 8),
             dma(3),
             dma(2),
             dma(2),
-            dma(4),
-            dma(4),
+            dma(5),
+            dma(5),
             dma(chips),
             dma(chips),
             dma(HALF),

time: 25.7 us -> 25.5 us (level)
  no operation moved by 1% of the time
where the time goes in v7:
time: 25.5 us
  Pallas kernels  25.4 us (100%)
    pallas_call x1, Pallas kernels, body(): pl.pallas_call(functools.partial(columns_kernel, n_h, n_d), out_shape=(V(...  23.6 us
    pallas_call x1, Pallas kernels, body(): pl.pallas_call(assemble_kernel, out_shape=jax.ShapeDtypeStruct(fields.sha...  1.87 us

profile of v7, /device:TPU:1, one launch (start us, length us, event | category | flops | bytes accessed | tf_op | source)
XLA Modules:
  0.0 25.5 jit_solution(9469277879155209182)
XLA Ops:
  0.0 23.6 %columns.1 = (f32[32,6,32,128]{3,2,1,0:T(8,128)S(1)}, f32[26,16,128]{2,1,0:T(8,128)S(1)}, f32[32,32,128]{2,1,0:T(8,128)S(1)}, f32[32,32,128]{2,1,0:T(8,128)S(1)}) custom-call(f32[3,32,32,256]{3,2,1,0:T(8,128)} %fields.1, f32[32,32,256]{2,1,0:T(8,128)} %diff.1, s32[32]{0:T(128)} %offs.1, f32[4,32]{1,0:T(4,128)} %coup.1, f32[4,32,32]{2,1,0:T(8,128)} %inv.1), custom_call_target="tpu_custom_call" | custom-call | tf_op jit(solution)/shard_map/columns/pallas_call | solution.py:652
  23.6 1.9 %assemble.1 = f32[3,32,32,256]{3,2,1,0:T(8,128)} custom-call(f32[32,6,32,128]{3,2,1,0:T(8,128)S(1)} %get-tuple-element.9.sol, f32[26,16,128]{2,1,0:T(8,128)S(1)} %get-tuple-element.10.back, f32[32,32,128]{2,1,0:T(8,128)S(1)} %get-tuple-element.11.low, f32[32,32,128]{2,1,0:T(8,128)S(1)} %get-tuple-element.12.high), custom_call_target="tpu_custom_call" | custom-call | tf_op jit(solution)/shard_map/assemble/pallas_call | solution.py:718

commit v8 on v7

--- a/solution.py
+++ b/solution.py
@@ -235,7 +235,7 @@
             for q in range(6):
                 m1[g * 6 + q, 8 * w:8 * w + 8, :] = sums[w * 6 + q]
 
-    def slot_forcing(slot, first):
+    def slot_forcing(slot, first, start, stop):
         def step_chunk(c, carry):
             if first:
                 for copy in chunk_copies(c):
@@ -244,12 +244,12 @@
                 forcing(c, g)
             return carry
 
-        lax.fori_loop(0, CHUNKS, step_chunk, 0)
+        lax.fori_loop(start, stop, step_chunk, 0)
 
     for slot in range(2):
         @pl.when(core == 1 - slot)
         def _():
-            slot_forcing(slot, True)
+            slot_forcing(slot, True, 0, CHUNKS)
 
     pair_coef = remote(cmsg, cpart, pair_send.at[0], pair_recv.at[0], partner)
     pair_rows = remote(m1.at[pl.ds((1 - core) * HALF, HALF)], other, pair_send.at[1], pair_recv.at[1], partner)
@@ -265,10 +265,13 @@
 
     for copy in (pair_coef, pair_rows):
         copy.start()
-    for slot in range(2):
-        @pl.when(core == slot)
-        def _():
-            slot_forcing(slot, False)
+    def second_half(start, stop):
+        for slot in range(2):
+            @pl.when(core == slot)
+            def _():
+                slot_forcing(slot, False, start, stop)
+
+    second_half(0, CHUNKS - 1)
 
     def splat(tile, at):
         return jnp.broadcast_to(tile[:, at:at + 1], (8, 128))
@@ -294,6 +297,8 @@
 
     for j, step in enumerate(steps):
         coef_copy(j, chip_at(step)).start()
+
+    second_half(CHUNKS - 1, CHUNKS)
 
     def one(ref, line):
         return jnp.broadcast_to(ref[line:line + 1, :], (8, 128))

time: 25.5 us -> 25.7 us (level)
  no operation moved by 1% of the time
where the time goes in v8:
time: 25.7 us; the launch traced here: 25.6 us
  Pallas kernels  25.6 us (100%)
    pallas_call x1, Pallas kernels, body(): pl.pallas_call(functools.partial(columns_kernel, n_h, n_d), out_shape=(V(...  23.7 us
    pallas_call x1, Pallas kernels, body(): pl.pallas_call(assemble_kernel, out_shape=jax.ShapeDtypeStruct(fields.sha...  1.87 us

profile of v8, /device:TPU:1, one launch (start us, length us, event | category | flops | bytes accessed | tf_op | source)
XLA Modules:
  0.0 25.6 jit_solution(15925334737875586481)
XLA Ops:
  0.0 23.7 %columns.1 = (f32[32,6,32,128]{3,2,1,0:T(8,128)S(1)}, f32[26,16,128]{2,1,0:T(8,128)S(1)}, f32[32,32,128]{2,1,0:T(8,128)S(1)}, f32[32,32,128]{2,1,0:T(8,128)S(1)}) custom-call(f32[3,32,32,256]{3,2,1,0:T(8,128)} %fields.1, f32[32,32,256]{2,1,0:T(8,128)} %diff.1, s32[32]{0:T(128)} %offs.1, f32[4,32]{1,0:T(4,128)} %coup.1, f32[4,32,32]{2,1,0:T(8,128)} %inv.1), custom_call_target="tpu_custom_call" | custom-call | tf_op jit(solution)/shard_map/columns/pallas_call | solution.py:657
  23.8 1.9 %assemble.1 = f32[3,32,32,256]{3,2,1,0:T(8,128)} custom-call(f32[32,6,32,128]{3,2,1,0:T(8,128)S(1)} %get-tuple-element.9.sol, f32[26,16,128]{2,1,0:T(8,128)S(1)} %get-tuple-element.10.back, f32[32,32,128]{2,1,0:T(8,128)S(1)} %get-tuple-element.11.low, f32[32,32,128]{2,1,0:T(8,128)S(1)} %get-tuple-element.12.high), custom_call_target="tpu_custom_call" | custom-call | tf_op jit(solution)/shard_map/assemble/pallas_call | solution.py:723
